TPU v7x, 256 devices: a 2x2x32 block of a 4x8x32 slice. The times are simulated.
256 devices in a mesh: ens: 4 (over y, x), region: 64 (over z, core).
Axes of the slice: x: 2, y: 2, z: 32, core: 2. Of those that a mesh axis runs over, the one named last changes fastest.
The devices are a block of a 4x8x32 slice.
Arguments:
- node_latent: bfloat16 [131072, 512], P(('ens', 'region')), parts along dimension 0, may hold values from -6 to 6
- grid_latent: bfloat16 [131072, 512], P(('ens', 'region')), parts along dimension 0, may hold values from -6 to 6
- fine_edge_sender: int32 [524288], P(('ens', 'region')), parts along dimension 0, may hold values from 0 to 32767, as said below
- short_recv: int32 [524288], P(('ens', 'region')), parts along dimension 0, may hold values from 0 to 511
- short_geo: float32 [4, 524288], P(None, ('ens', 'region')), parts along dimension 1, may hold values from -6 to 6
- long_send: int32 [131072], P(('ens', 'region')), parts along dimension 0, may hold values from -1 to 32767, as said below
- long_recv: int32 [131072], P(('ens', 'region')), parts along dimension 0, may hold values from 0 to 511
- long_geo: float32 [4, 131072], P(None, ('ens', 'region')), parts along dimension 1, may hold values from -6 to 6
- dec_send: int32 [3, 131072], P(None, ('ens', 'region')), parts along dimension 1, may hold values from 0 to 32767, as said below
- dec_geo: float32 [4, 3, 131072], P(None, None, ('ens', 'region')), parts along dimension 2, may hold values from -6 to 6
- w_send: bfloat16 [512, 512], replicated, may hold values from -0.25 to 0.25
- w_recv: bfloat16 [512, 512], replicated, may hold values from -0.25 to 0.25
- w_edge_geo: float32 [4, 512], replicated, may hold values from -3 to 3
- w_message: bfloat16 [512, 512], replicated, may hold values from -0.25 to 0.25
- w_node_self: bfloat16 [512, 512], replicated, may hold values from -0.25 to 0.25
- w_node_agg: bfloat16 [512, 512], replicated, may hold values from -0.25 to 0.25
- w_node_out: bfloat16 [512, 512], replicated, may hold values from -0.25 to 0.25
- w_dec_send: bfloat16 [512, 512], replicated, may hold values from -0.25 to 0.25
- w_dec_grid: bfloat16 [512, 512], replicated, may hold values from -0.25 to 0.25
- w_dec_geo: float32 [4, 512], replicated, may hold values from -3 to 3
- decoding_link_final_matrix: bfloat16 [512, 512], replicated, may hold values from -0.25 to 0.25
- w_grid_agg: bfloat16 [512, 512], replicated, may hold values from -0.25 to 0.25
- w_grid_self: bfloat16 [512, 512], replicated, may hold values from -0.25 to 0.25
- final_projection_matrix: bfloat16 [100, 512], replicated, may hold values from -0.25 to 0.25
Outputs:
- refreshed_mesh_latents: bfloat16 [131072, 512], P(('ens', 'region')), parts along dimension 0
- predicted_fields: bfloat16 [100, 131072], P(None, ('ens', 'region')), parts along dimension 1
There are 4 independent parts, one for each index of `ens`. A program takes and returns all parts, laid end to end along the dimension named above; an argument that names none is the same for every part. Nothing has to cross between parts.
Inputs may be any that keep to these rules, and one draw needn't show every extreme that they name: `fine_edge_sender`: A fine edge held by region d has its sender in region d, among the last 64 nodes of region d - 1, or among the first 64 nodes of region d + 1; node 448 of region d - 1 (the first of its last 64) and node 63 of region d + 1 are used where those regions exist. `long_send`: slot d * 512 + o * 8 + j, unless -1, names one of the first 64 nodes of region o; in every region one other region's 8 slots are all filled. `dec_send`: the senders of a grid point of band d lie in region d, among the last 64 nodes of region d - 1, or among the first 64 nodes of region d + 1; node 448 of region d - 1 (the first of its last 64) and node 63 of region d + 1 are used where those regions exist.
All inputs are finite; a program needn't handle non-finite values.
Results may differ from a plain program's by a relative error of at most 0.013.
Values may be sent and summed in bfloat16 or wider, within the bound.
No kernel may reach another device: no remote copies, remote signals or barrier semaphores. Data moves between devices by JAX's collectives and lax.ppermute only.
A program may use at most 128 MiB of HBM per device.

v0:
```python
import jax
import jax.numpy as jnp
from jax import lax
from jax.sharding import PartitionSpec as P

BORDER = 64


def extended_2(array, sides, width):
    for axis, dim in sides:
        size, length = (lax.axis_size(axis), array.shape[dim])
        up = [(i, (i + 1) % size) for i in range(size - 1)]
        down = [(j, i) for i, j in up]
        last = lax.slice_in_dim(array, length - width, length, axis=dim)
        initial = lax.slice_in_dim(array, 0, width, axis=dim)
        before = lax.ppermute(last, axis, up)
        after = lax.ppermute(initial, axis, down)
        array = jnp.concatenate([before, array, after], axis=dim)
    return array


def product(left, right):
    return jnp.dot(left, right, preferred_element_type=jnp.float32)


def geometry(feature_vectors, learned_factor):
    return lax.dot_general(
        feature_vectors, learned_factor, (((0,), (0,)), ((), ())), precision=lax.Precision.HIGHEST
    )


def normalize(values):
    middle_point = values - jnp.mean(values, axis=-1, keepdims=True)
    spread = jnp.mean(middle_point * middle_point, axis=-1, keepdims=True)
    return middle_point * lax.rsqrt(spread + 1e-05)


def messages(edge_pre, w_message):
    edge_hidden = jax.nn.silu(edge_pre).astype(jnp.bfloat16)
    return normalize(product(edge_hidden, w_message))


def body(
    node_latent,
    grid_latent,
    fine_edge_sender,
    short_recv,
    short_geo,
    long_send,
    long_recv,
    long_geo,
    dec_send,
    dec_geo,
    w_send,
    w_recv,
    w_edge_geo,
    w_message,
    w_node_self,
    w_node_agg,
    w_node_out,
    w_dec_send,
    w_dec_grid,
    w_dec_geo,
    decoding_link_final_matrix,
    w_grid_agg,
    w_grid_self,
    final_projection_matrix,
):
    node_count = node_latent.shape[0]
    channel_count = node_latent.shape[1]
    region = lax.axis_index("region")
    row_offset = region * node_count - BORDER
    extended = extended_2(node_latent, (("region", 0),), BORDER)
    send_ext = product(extended, w_send)
    recv_proj = product(node_latent, w_recv)
    fine_pre = (
        send_ext[fine_edge_sender - row_offset]
        + recv_proj[short_recv]
        + geometry(short_geo, w_edge_geo)
    )
    fine_msg = messages(fine_pre, w_message)
    present = long_send >= 0
    clipped = jnp.maximum(long_send, 0)
    owner = clipped // node_count
    within = clipped - owner * node_count
    regions = lax.axis_size("region")
    asked = within.reshape(regions, -1)
    fetched = lax.all_to_all(
        node_latent[lax.all_to_all(asked, "region", split_axis=0, concat_axis=0, tiled=True)],
        "region",
        split_axis=0,
        concat_axis=0,
        tiled=True,
    ).reshape(-1, channel_count)
    far_pre = product(fetched, w_send) + recv_proj[long_recv] + geometry(long_geo, w_edge_geo)
    far_msg = messages(far_pre, w_message) * present[:, None].astype(jnp.float32)
    aggregate = (
        jnp.zeros((node_count, channel_count), jnp.float32)
        .at[short_recv]
        .add(fine_msg)
        .at[long_recv]
        .add(far_msg)
    )
    node_hidden = jax.nn.silu(
        product(node_latent, w_node_self) + product(aggregate.astype(jnp.bfloat16), w_node_agg)
    ).astype(jnp.bfloat16)
    refreshed_mesh_latents = (
        node_latent.astype(jnp.float32) + product(node_hidden, w_node_out)
    ).astype(jnp.bfloat16)
    updated_extended = extended_2(refreshed_mesh_latents, (("region", 0),), BORDER)
    dec_proj = product(updated_extended, w_dec_send)
    grid_proj = product(grid_latent, w_dec_grid)
    grid_sum = jnp.zeros(grid_proj.shape, jnp.float32)
    for vertex in range(3):
        dec_pre = (
            dec_proj[dec_send[vertex] - row_offset]
            + grid_proj
            + geometry(dec_geo[:, vertex, :], w_dec_geo)
        )
        grid_sum = grid_sum + messages(dec_pre, decoding_link_final_matrix)
    grid_agg = grid_sum.astype(jnp.bfloat16)
    latitude_site_latent_matrix = jax.nn.silu(
        product(grid_agg, w_grid_agg) + product(grid_latent, w_grid_self)
    ).astype(jnp.bfloat16)
    predicted_fields = lax.dot_general(
        final_projection_matrix,
        latitude_site_latent_matrix,
        (((1,), (1,)), ((), ())),
        preferred_element_type=jnp.float32,
    ).astype(jnp.bfloat16)
    return (refreshed_mesh_latents, predicted_fields)


def solution(mesh):
    in_specs = (
        P(("ens", "region"), None),
        P(("ens", "region"), None),
        P(("ens", "region")),
        P(("ens", "region")),
        P(None, ("ens", "region")),
        P(("ens", "region")),
        P(("ens", "region")),
        P(None, ("ens", "region")),
        P(None, ("ens", "region")),
        P(None, None, ("ens", "region")),
        P(),
        P(),
        P(),
        P(),
        P(),
        P(),
        P(),
        P(),
        P(),
        P(),
        P(),
        P(),
        P(),
        P(),
    )
    out_specs = (P(("ens", "region"), None), P(None, ("ens", "region")))
    return jax.shard_map(body, mesh=mesh, in_specs=in_specs, out_specs=out_specs, check_vma=False)
```

profile of v0, /device:TPU:37, one launch (start us, length us, event | category | flops | bytes accessed | tf_op | source)
XLA Modules:
  0.0 194.6 jit_solution(13271283803165956613)
XLA Ops:
  1.6 5.1 %collective-permute-start = (bf16[64,512]{1,0:T(8,128)(2,1)S(1)}, bf16[64,512]{1,0:T(8,128)(2,1)S(1)}, u32[]{:S(2)}, u32[]{:S(2)}) collective-permute-start(bf16[64,512]{1,0:T(8,128)(2,1)S(1)} %get-tuple-element.4), channel_id=1, source_target_pairs={{0,1},{1,2},{2,3},{3,4},{4,5},{5,6},{6,7},{7,8},{8,9},{9,10},{10,1... | collective-permute-start | bytes 196616 | tf_op jit(solution)/shard_map/ppermute | solution.py:16
  6.7 18.6 %collective-permute-start.1 = (bf16[64,512]{1,0:T(8,128)(2,1)S(1)}, bf16[64,512]{1,0:T(8,128)(2,1)}, u32[]{:S(2)}, u32[]{:S(2)}) collective-permute-start(bf16[64,512]{1,0:T(8,128)(2,1)S(1)} %get-tuple-element.5), channel_id=1, source_target_pairs={{1,0},{2,1},{3,2},{4,3},{5,4},{6,5},{7,6},{8,7},{9,8},{10,9},{11,1... | collective-permute-start | bytes 196616 | tf_op jit(solution)/shard_map/ppermute | solution.py:17
  26.7 17.5 %all-to-all-start = ((s32[64,1,8]{2,1,0:T(1,128)}), s32[64,1,8]{2,1,0:T(1,128)S(1)}, u32[]{:S(2)}, u32[]{:S(2)}) async-start(s32[64,1,8]{2,1,0:T(1,128)} %bitcast), calls=%async_computation | async-start | bytes 65536 | tf_op jit(solution)/shard_map/all_to_all | solution.py:89
  48.1 8.9 %gather_fusion.1 = f32[2048,512]{1,0:T(8,128)} fusion(f32[512,512]{1,0:T(8,128)S(1)} %fusion.52, s32[2048]{0:T(1024)S(1)} %get-tuple-element.9), kind=kCustom, calls=%fused_computation.1 | custom fusion | bytes 8396800 | tf_op jit(solution)/shard_map/gather | solution.py:78
  58.6 7.5 %all-to-all-done = s32[64,1,8]{2,1,0:T(1,128)S(1)} async-done(((s32[64,1,8]{2,1,0:T(1,128)}), s32[64,1,8]{2,1,0:T(1,128)S(1)}, u32[]{:S(2)}, u32[]{:S(2)}) %all-to-all-start) | async-done | bytes 2080 | tf_op jit(solution)/shard_map/all_to_all | solution.py:89
  66.3 2.6 %gather_fusion.2 = bf16[512,512]{1,0:T(8,128)(2,1)} fusion(bf16[512,512]{1,0:T(8,128)(2,1)S(1)} %copy-done.1, s32[1024]{0:T(1024)S(1)} %pad_clamp_fusion.4), kind=kCustom, calls=%fused_computation.2 | custom fusion | bytes 1050624 | tf_op jit(solution)/shard_map/gather | solution.py:89
  68.9 15.8 %all-to-all-start.1 = ((bf16[64,8,512]{2,1,0:T(8,128)(2,1)}), bf16[64,8,512]{2,1,0:T(8,128)(2,1)}, u32[]{:S(2)}, u32[]{:S(2)}) async-start(bf16[64,8,512]{2,1,0:T(8,128)(2,1)} %bitcast.2), calls=%async_computation.1 | async-start | bytes 1048576 | tf_op jit(solution)/shard_map/all_to_all | solution.py:88
  86.2 2.5 %fusion.54 = f32[512,512]{1,0:T(8,128)} fusion(bf16[512,512]{1,0:T(8,128)(2,1)} %param.25, bf16[512,512]{1,0:T(8,128)(2,1)S(1)} %copy-done.5), kind=kOutput, calls=%fused_computation.113 | convolution fusion | flops 268435456 | bytes 2097152 | tf_op jit(solution)/shard_map/dot_general | solution.py:23
  88.7 5.1 %fusion.53 = f32[2048,512]{1,0:T(8,128)} fusion(f32[4,2048]{1,0:T(4,128)S(1)} %copy-done.9, f32[4,512]{1,0:T(4,128)S(1)} %copy-done.11), kind=kOutput, calls=%fused_computation.112 | convolution fusion | flops 50331648 | bytes 4235264 | tf_op jit(solution)/shard_map/dot_general | solution.py:27
  95.2 9.0 %gather_fusion = f32[2048,512]{1,0:T(8,128)} fusion(f32[640,512]{1,0:T(8,128)S(1)} %fusion.3, s32[2048]{0:T(1024)S(1)} %fusion.29), kind=kCustom, calls=%fused_computation | custom fusion | bytes 8396800 | tf_op jit(solution)/shard_map/gather | solution.py:77
  104.1 6.4 %fusion.46 = (f32[2048]{0:T(1024)S(1)}, f32[2048,512]{0,1:T(8,128)S(1)}) fusion(bf16[512,512]{1,0:T(8,128)(2,1)S(1)} %copy-done, f32[2048,512]{1,0:T(8,128)} %fusion.53, f32[2048,512]{1,0:T(8,128)} %gather_fusion, f32[2048,512]{1,0:T(8,128)} %gather_fusion.1), kind=kOutput, calls=%fused_computation.105 | convolution fusion | flops 1082128384 | bytes 17309696 | tf_op jit(solution)/shard_map/dot_general | solution.py:23
  111.1 2.4 %subtract_multiply_fusion = f32[2048,512]{0,1:T(8,128)} fusion(f32[2048,512]{0,1:T(8,128)S(1)} %get-tuple-element.12, f32[2048]{0:T(1024)S(1)} %add_rsqrt_fusion, f32[2048]{0:T(1024)S(1)} %broadcast_multiply_fusion), kind=kLoop, calls=%fused_computation.11 | loop fusion | flops 2097152 | bytes 8404992 | tf_op jit(solution)/shard_map/mul | solution.py:35
  113.6 5.4 %copy.28 = f32[2048,512]{1,0:T(8,128)} copy(f32[2048,512]{0,1:T(8,128)} %subtract_multiply_fusion) | data formatting | bytes 8388608 | tf_op jit(solution)/shard_map/mul | solution.py:35
  118.9 13.5 %scatter_custom_fusion = f32[512,512]{1,0:T(8,128)S(1)} fusion(s32[2048]{0:T(1024)S(1)} %get-tuple-element.10, f32[2048,512]{1,0:T(8,128)} %copy.28, f32[]{:T(128)} %constant.51.clone.1), kind=kCustom, calls=%fused_computation.59 | custom fusion | flops 1048576 | bytes 1049088 | tf_op jit(solution)/shard_map/scatter-add | solution.py:100
  132.4 16.3 %all-to-all-done.1 = bf16[64,8,512]{2,1,0:T(8,128)(2,1)} async-done(((bf16[64,8,512]{2,1,0:T(8,128)(2,1)}), bf16[64,8,512]{2,1,0:T(8,128)(2,1)}, u32[]{:S(2)}, u32[]{:S(2)}) %all-to-all-start.1) | async-done | bytes 524320 | tf_op jit(solution)/shard_map/all_to_all | solution.py:88
  155.0 4.2 %scatter_fusion = f32[512,512]{1,0:T(8,128)S(1)} fusion(f32[512,512]{1,0:T(8,128)S(1)} %scatter_custom_fusion, s32[512]{0:T(512)S(1)} %compare_select_fusion.6, f32[512,512]{1,0:T(8,128)S(1)} %copy.30), kind=kCustom, calls=%fused_computation.8 | custom fusion | flops 262144 | bytes 3147776 | tf_op jit(solution)/shard_map/scatter-add | solution.py:102
  159.2 2.4 %fusion.1 = bf16[512,512]{1,0:T(8,128)(2,1)S(1)} fusion(bf16[512,512]{1,0:T(8,128)(2,1)} %param.40, f32[512,512]{1,0:T(8,128)} %fusion.51, bf16[512,512]{1,0:T(8,128)(2,1)} %param.39, bf16[512,512]{1,0:T(8,128)(2,1)S(1)} %copy-done.1, f32[512,512]{1,0:T(8,128)S(1)} %scatter_fusion), kind=kOutput, calls=%fused_computation.21 | convolution fusion | flops 539492352 | bytes 4194304 | tf_op jit(solution)/shard_map/dot_general | solution.py:23
  161.6 3.6 %collective-permute-start.2 = (bf16[64,512]{1,0:T(8,128)(2,1)S(1)}, bf16[64,512]{1,0:T(8,128)(2,1)S(1)}, u32[]{:S(2)}, u32[]{:S(2)}) collective-permute-start(bf16[64,512]{1,0:T(8,128)(2,1)S(1)} %get-tuple-element.2), channel_id=1, source_target_pairs={{0,1},{1,2},{2,3},{3,4},{4,5},{5,6},{6,7},{7,8},{8,9},{9,10},{10,1... | collective-permute-start | bytes 196616 | tf_op jit(solution)/shard_map/ppermute | solution.py:16
  167.2 3.6 %collective-permute-done.3 = bf16[64,512]{1,0:T(8,128)(2,1)S(1)} collective-permute-done((bf16[64,512]{1,0:T(8,128)(2,1)S(1)}, bf16[64,512]{1,0:T(8,128)(2,1)S(1)}, u32[]{:S(2)}, u32[]{:S(2)}) %collective-permute-start.3) | collective-permute-done | bytes 65568 | tf_op jit(solution)/shard_map/ppermute | solution.py:17
  174.1 2.5 %multiply_convert_fusion.5 = bf16[512,512]{1,0:T(8,128)(2,1)S(1)} fusion(f32[4,512]{1,0:T(4,128)S(1)} %copy-done.17, f32[512,512]{1,0:T(8,128)S(1)} %gather_fusion.4, f32[512,512]{1,0:T(8,128)} %fusion.54, f32[4,3,512]{2,0,1:T(4,128)S(1)} %copy-done.15), kind=kOutput, calls=%fused_computation.31 | convolution fusion | flops 14417920 | bytes 2637824 | tf_op jit(solution)/shard_map/dot_general | solution.py:27
  177.3 2.3 %gather_fusion.5 = f32[512,512]{1,0:T(8,128)} fusion(f32[640,512]{1,0:T(8,128)S(1)} %fusion.9, s32[1024]{0:T(1024)S(1)} %pad_clamp_fusion.1), kind=kCustom, calls=%fused_computation.5 | custom fusion | bytes 2099200 | tf_op jit(solution)/shard_map/gather | solution.py:116
  179.7 2.7 %multiply_convert_fusion.4 = bf16[512,512]{1,0:T(8,128)(2,1)S(1)} fusion(f32[4,512]{1,0:T(4,128)S(1)} %copy-done.17, f32[512,512]{1,0:T(8,128)} %gather_fusion.5, f32[512,512]{1,0:T(8,128)} %fusion.54, f32[4,3,512]{2,0,1:T(4,128)S(1)} %copy-done.15), kind=kOutput, calls=%fused_computation.29 | convolution fusion | flops 14417920 | bytes 2637824 | tf_op jit(solution)/shard_map/dot_general | solution.py:27
  186.2 2.9 %multiply_convert_fusion.3 = bf16[512,512]{1,0:T(8,128)(2,1)S(1)} fusion(f32[4,512]{1,0:T(4,128)S(1)} %copy-done.17, f32[512,512]{1,0:T(8,128)} %gather_fusion.6, f32[512,512]{1,0:T(8,128)} %fusion.54, f32[4,3,512]{2,0,1:T(4,128)S(1)} %copy-done.15), kind=kOutput, calls=%fused_computation.27 | convolution fusion | flops 14417920 | bytes 2637824 | tf_op jit(solution)/shard_map/dot_general | solution.py:27
  191.7 2.8 %fusion.2 = bf16[100,512]{1,0:T(8,128)(2,1)} fusion(bf16[100,512]{1,0:T(8,128)(2,1)S(1)} %copy-done.14, f32[512,512]{1,0:T(8,128)} %fusion.15, bf16[512,512]{1,0:T(8,128)(2,1)S(1)} %copy-done.7, bf16[512,512]{1,0:T(8,128)(2,1)} %param.46), kind=kOutput, calls=%fused_computation.23 | convolution fusion | flops 322488320 | bytes 2301952 | tf_op jit(solution)/shard_map/dot_general | solution.py:125
  (86 shorter events, 29.7 us)
Async XLA Ops:
  0.6 103.5 %copy-start = (bf16[512,512]{1,0:T(8,128)(2,1)S(1)}, bf16[512,512]{1,0:T(8,128)(2,1)}, u32[]{:S(2)}) copy-start(bf16[512,512]{1,0:T(8,128)(2,1)} %param.37) | copy-start | bytes 1572868
  1.6 92.2 %collective-permute-start = (bf16[64,512]{1,0:T(8,128)(2,1)S(1)}, bf16[64,512]{1,0:T(8,128)(2,1)S(1)}, u32[]{:S(2)}, u32[]{:S(2)}) collective-permute-start(bf16[64,512]{1,0:T(8,128)(2,1)S(1)} %get-tuple-element.4), channel_id=1, source_target_pairs={{0,1},{1,2},{2,3},{3,4},{4,5},{5,6},{6,7},{7,8},{8,9},{9,10},{10,1... | collective-permute-start | bytes 196616 | tf_op jit(solution)/shard_map/ppermute | solution.py:16
  6.7 87.1 %collective-permute-start.1 = (bf16[64,512]{1,0:T(8,128)(2,1)S(1)}, bf16[64,512]{1,0:T(8,128)(2,1)}, u32[]{:S(2)}, u32[]{:S(2)}) collective-permute-start(bf16[64,512]{1,0:T(8,128)(2,1)S(1)} %get-tuple-element.5), channel_id=1, source_target_pairs={{1,0},{2,1},{3,2},{4,3},{5,4},{6,5},{7,6},{8,7},{9,8},{10,9},{11,1... | collective-permute-start | bytes 196616 | tf_op jit(solution)/shard_map/ppermute | solution.py:17
  26.7 39.5 %all-to-all-start = ((s32[64,1,8]{2,1,0:T(1,128)}), s32[64,1,8]{2,1,0:T(1,128)S(1)}, u32[]{:S(2)}, u32[]{:S(2)}) async-start(s32[64,1,8]{2,1,0:T(1,128)} %bitcast), calls=%async_computation | async-start | bytes 65536 | tf_op jit(solution)/shard_map/all_to_all | solution.py:89
  57.0 9.3 %copy-start.1 = (bf16[512,512]{1,0:T(8,128)(2,1)S(1)}, bf16[512,512]{1,0:T(8,128)(2,1)}, u32[]{:S(2)}) copy-start(bf16[512,512]{1,0:T(8,128)(2,1)} %param.24) | copy-start | bytes 1572868
  58.6 26.1 %copy-start.13 = (s32[512]{0:T(512)S(1)}, s32[512]{0:T(512)}, u32[]{:S(2)}) copy-start(s32[512]{0:T(512)} %param.29) | copy-start | bytes 6148
  58.6 26.1 %copy-start.12 = (s32[2048]{0:T(1024)S(1)}, s32[2048]{0:T(1024)}, u32[]{:S(2)}) copy-start(s32[2048]{0:T(1024)} %param.26) | copy-start | bytes 24580
  58.6 26.2 %copy-start.4 = (bf16[512,512]{1,0:T(8,128)(2,1)S(1)}, bf16[512,512]{1,0:T(8,128)(2,1)}, u32[]{:S(2)}) copy-start(bf16[512,512]{1,0:T(8,128)(2,1)} %param.38) | copy-start | bytes 1572868
  58.6 27.6 %copy-start.5 = (bf16[512,512]{1,0:T(8,128)(2,1)S(1)}, bf16[512,512]{1,0:T(8,128)(2,1)}, u32[]{:S(2)}) copy-start(bf16[512,512]{1,0:T(8,128)(2,1)} %param.42) | copy-start | bytes 1572868
  66.3 22.4 %copy-start.9 = (f32[4,2048]{1,0:T(4,128)S(1)}, f32[4,2048]{1,0:T(4,128)}, u32[]{:S(2)}) copy-start(f32[4,2048]{1,0:T(4,128)} %param.28) | copy-start | bytes 98308
  66.3 22.4 %copy-start.11 = (f32[4,512]{1,0:T(4,128)S(1)}, f32[4,512]{1,0:T(4,128)}, u32[]{:S(2)}) copy-start(f32[4,512]{1,0:T(4,128)} %param.36) | copy-start | bytes 24580
  68.9 79.8 %all-to-all-start.1 = ((bf16[64,8,512]{2,1,0:T(8,128)(2,1)}), bf16[64,8,512]{2,1,0:T(8,128)(2,1)}, u32[]{:S(2)}, u32[]{:S(2)}) async-start(bf16[64,8,512]{2,1,0:T(8,128)(2,1)} %bitcast.2), calls=%async_computation.1 | async-start | bytes 1048576 | tf_op jit(solution)/shard_map/all_to_all | solution.py:88
  84.8 9.0 %copy-start.6 = (bf16[512,512]{1,0:T(8,128)(2,1)S(1)}, bf16[512,512]{1,0:T(8,128)(2,1)}, u32[]{:S(2)}) copy-start(bf16[512,512]{1,0:T(8,128)(2,1)} %param.34) | copy-start | bytes 1572868
  118.9 31.4 %copy-start.16 = (f32[4,512]{1,0:T(4,128)S(1)}, f32[4,512]{1,0:T(4,128)}, u32[]{:S(2)}) copy-start(f32[4,512]{1,0:T(4,128)} %param.31) | copy-start | bytes 24580
  161.6 9.3 %copy-start.10 = (bf16[512,512]{1,0:T(8,128)(2,1)}, bf16[512,512]{1,0:T(8,128)(2,1)S(1)}, u32[]{:S(2)}) copy-start(bf16[512,512]{1,0:T(8,128)(2,1)S(1)} %fusion.1) | copy-start | bytes 1572868
  161.6 5.6 %collective-permute-start.2 = (bf16[64,512]{1,0:T(8,128)(2,1)S(1)}, bf16[64,512]{1,0:T(8,128)(2,1)S(1)}, u32[]{:S(2)}, u32[]{:S(2)}) collective-permute-start(bf16[64,512]{1,0:T(8,128)(2,1)S(1)} %get-tuple-element.2), channel_id=1, source_target_pairs={{0,1},{1,2},{2,3},{3,4},{4,5},{5,6},{6,7},{7,8},{8,9},{9,10},{10,1... | collective-permute-start | bytes 196616 | tf_op jit(solution)/shard_map/ppermute | solution.py:16
  165.3 5.6 %collective-permute-start.3 = (bf16[64,512]{1,0:T(8,128)(2,1)S(1)}, bf16[64,512]{1,0:T(8,128)(2,1)S(1)}, u32[]{:S(2)}, u32[]{:S(2)}) collective-permute-start(bf16[64,512]{1,0:T(8,128)(2,1)S(1)} %get-tuple-element.3), channel_id=1, source_target_pairs={{1,0},{2,1},{3,2},{4,3},{5,4},{6,5},{7,6},{8,7},{9,8},{10,9},{11,1... | collective-permute-start | bytes 196616 | tf_op jit(solution)/shard_map/ppermute | solution.py:17
  172.4 1.7 copy-start.15
  172.4 1.7 copy-start.17
  174.1 2.5 %copy-start.3 = (bf16[512,512]{1,0:T(8,128)(2,1)S(1)}, bf16[512,512]{1,0:T(8,128)(2,1)}, u32[]{:S(2)}) copy-start(bf16[512,512]{1,0:T(8,128)(2,1)} %param.44) | copy-start | bytes 1572868
  186.2 3.4 %copy-start.2 = (f32[512,512]{0,1:T(8,128)S(1)}, f32[512,512]{0,1:T(8,128)}, u32[]{:S(2)}) copy-start(f32[512,512]{0,1:T(8,128)} %get-tuple-element.18) | copy-start | bytes 3145732
  186.2 3.8 %copy-start.8 = (bf16[512,512]{1,0:T(8,128)(2,1)S(1)}, bf16[512,512]{1,0:T(8,128)(2,1)}, u32[]{:S(2)}) copy-start(bf16[512,512]{1,0:T(8,128)(2,1)} %param.45) | copy-start | bytes 1572868
  189.1 2.6 %copy-start.14 = (bf16[100,512]{1,0:T(8,128)(2,1)S(1)}, bf16[100,512]{1,0:T(8,128)(2,1)}, u32[]{:S(2)}) copy-start(bf16[100,512]{1,0:T(8,128)(2,1)} %param.47) | copy-start | bytes 307204
  189.6 2.1 %copy-start.7 = (bf16[512,512]{1,0:T(8,128)(2,1)S(1)}, bf16[512,512]{1,0:T(8,128)(2,1)}, u32[]{:S(2)}) copy-start(bf16[512,512]{1,0:T(8,128)(2,1)} %param.25) | copy-start | bytes 1572868
where the time goes:
time: 195 us
  starting transfers between devices  62.5 us (32%)
  matrix products  40.7 us (21%)
  local copies, waits for them, and re-layouts  37.2 us (19%)
  waiting for transfers between devices  27.4 us (14%)
  other arithmetic  25.5 us (13%)
    dot_general x13, matrix products, product(): return jnp.dot(left, right, preferred_element_type=jnp.float32)  23.5 us
    ppermute x2, starting transfers between devices, extended_2(): after = lax.ppermute(initial, axis, down)  20.5 us
    scatter-add x2, other arithmetic, body(): aggregate = jnp.zeros((node_count, channel_count), jnp.float32).at[short_...  17.7 us
    all_to_all x1, starting transfers between devices, body(): lax.all_to_all(asked, 'region', split_axis=0, concat_axis=0, tiled=True)  17.5 us
    all_to_all x1, waiting for transfers between devices, body(): lax.all_to_all(node_latent[lax.all_to_all(asked, 'region', split_axis=0,...  16.3 us
    all_to_all x1, starting transfers between devices, body(): lax.all_to_all(node_latent[lax.all_to_all(asked, 'region', split_axis=0,...  15.8 us
    dot_general x5, matrix products, geometry(): lax.dot_general(feature_vectors, learned_factor, (((0,), (0,)), ((), ()))...  14.4 us
    gather x1, local copies, waits for them, and re-layouts, body(): send_ext[fine_edge_sender - row_offset] + recv_proj[short_recv]  8.99 us
  transfers between devices with their start and end apart: 6, of which 3 were waited for; matrix products, arithmetic and copies ran while one was open for 34% of the time, Pallas kernels for 0%

commit v1 on v0

v1 whole, which is shorter than its diff:
```python
import functools

import jax
import jax.numpy as jnp
from jax import lax
from jax.experimental import pallas as pl
from jax.experimental.pallas import tpu as pltpu
from jax.sharding import PartitionSpec as P

BORDER = 64
COARSE = 64
BLOCK = 8
LANES = 128
F32 = jnp.float32
BF16 = jnp.bfloat16


def dot(left, right):
    return jnp.dot(left, right, preferred_element_type=F32)


def silu(v):
    half = 0.5 * v
    return half + half * jnp.tanh(half)


def normalize(values):
    inv = 1.0 / values.shape[-1]
    centred = values - jnp.sum(values, axis=-1, keepdims=True) * inv
    spread = jnp.sum(centred * centred, axis=-1, keepdims=True) * inv
    return centred * lax.rsqrt(spread + 1e-05)


def columns(rows):
    return jnp.concatenate(
        [jnp.broadcast_to(r, (LANES, LANES)).T for r in rows], axis=0
    )


def one_hot(cols, width):
    lane = lax.broadcasted_iota(jnp.int32, cols.shape, 1)
    return jnp.concatenate(
        [jnp.where(cols == lane + k, 1.0, 0.0).astype(BF16) for k in range(0, width, LANES)], axis=1
    )


def one_hot_t(rows, height):
    node = lax.broadcasted_iota(jnp.int32, (height, LANES), 0)
    return jnp.concatenate([jnp.where(node == r, 1.0, 0.0).astype(BF16) for r in rows], axis=1)


def split(values):
    high = values.astype(BF16).astype(F32)
    return high, values - high


def geo_columns(stack):
    n = stack.shape[1]
    full = jnp.concatenate([stack, jnp.zeros((LANES - 32, n), F32)], axis=0)
    return jnp.concatenate(
        [full[:, b : b + LANES].T for b in range(0, n, LANES)], axis=0
    ).astype(BF16)


def fill_geo(ref, first, second, third):
    ref[...] = jnp.zeros(ref.shape, F32)
    n = first.shape[0]
    ref[0:n, :] = first
    ref[8 : 8 + n, :] = second
    ref[16 : 16 + n, :] = third


def geo_table(wref, scratch):
    high, low = split(wref[...])
    fill_geo(scratch, high, high, low)
    rows = scratch[...]
    return jnp.concatenate([rows, jnp.zeros((LANES - 32, rows.shape[1]), F32)], axis=0).astype(BF16)


def fetch(pairs, sems):
    copies = [pltpu.make_async_copy(src, dst, sems.at[i]) for i, (src, dst) in enumerate(pairs)]
    for copy in copies:
        copy.start()
    return copies


def relay_kernel(asked_ref, table_ref, out_ref):
    rows = out_ref.shape[0] // asked_ref.shape[0]
    cols = jnp.concatenate(
        [columns([asked_ref[q, 0:1, :]])[:rows] for q in range(asked_ref.shape[0])], axis=0
    )
    out_ref[...] = dot(one_hot(cols, table_ref.shape[0]), table_ref[...]).astype(BF16)


def fine_kernel(
    off_ref, fs_ref, sr_ref, geo_ref, lr_ref, lgeo_ref, before_ref, after_ref, weg_ref,
    x_hbm, ws_hbm, wr_hbm, wm_hbm, wself_hbm,
    agg_ref, base_ref, nself_ref, ws_ref,
    tab, msg, gsc, lsc, wsc, x_ref, wr_ref, wm_ref, wself_ref, sems, *, tile,
):
    x_copy, ws_copy, wr_copy, wm_copy, wself_copy = fetch(
        [(x_hbm, x_ref), (ws_hbm, ws_ref), (wr_hbm, wr_ref), (wm_hbm, wm_ref), (wself_hbm, wself_ref)],
        sems,
    )
    n, h = x_ref.shape
    edges = geo_ref.shape[1]
    ext = n + 2 * BORDER
    tab[ext + n : ext + n + LANES, :] = geo_table(weg_ref, wsc)
    high, low = split(geo_ref[...])
    fill_geo(gsc, high, low, high)
    high, low = split(lgeo_ref[...])
    fill_geo(lsc, high, low, high)
    x_copy.wait()
    ws_copy.wait()
    x = x_ref[...]
    tab[0:BORDER, :] = dot(before_ref[...], ws_ref[...]).astype(BF16)
    tab[BORDER : BORDER + n, :] = dot(x, ws_ref[...]).astype(BF16)
    tab[BORDER + n : ext, :] = dot(after_ref[...], ws_ref[...]).astype(BF16)
    wr_copy.wait()
    tab[ext : ext + n, :] = dot(x, wr_ref[...]).astype(BF16)
    wself_copy.wait()
    nself_ref[...] = dot(x, wself_ref[...]).astype(BF16)
    wm_copy.wait()
    off = off_ref[0]
    per = tile // LANES

    def step(t, carry):
        row = t * per
        lane0 = pl.multiple_of(t * tile, tile)
        send = columns([fs_ref[pl.ds(row + b, 1), :] - off for b in range(per)])
        recv = columns([sr_ref[pl.ds(row + b, 1), :] for b in range(per)])
        lhs = jnp.concatenate(
            [one_hot(send, ext), one_hot(recv, n), geo_columns(gsc[:, pl.ds(lane0, tile)])], axis=1
        )
        hidden = silu(dot(lhs, tab[...])).astype(BF16)
        msg[pl.ds(lane0, tile), :] = normalize(dot(hidden, wm_ref[...])).astype(BF16)
        return carry

    lax.fori_loop(0, edges // tile, step, 0)
    agg_ref[...] = dot(
        one_hot_t([sr_ref[b : b + 1, :] for b in range(edges // LANES)], n), msg[...]
    )
    far = lr_ref.shape[0]
    recv = columns([lr_ref[b : b + 1, :] for b in range(far)])
    lhs = jnp.concatenate([one_hot(recv, n), geo_columns(lsc[...])], axis=1)
    base_ref[...] = dot(lhs, tab[ext : ext + n + LANES, :]).astype(BF16)


def node_kernel(
    lr_ref, far_ref, agg_ref, base_ref, nself_ref, ws_ref, x_hbm, wm_hbm, wa_hbm, wo_hbm,
    out_ref, first_ref, last_ref, x_ref, wm_ref, wa_ref, wo_ref, sems,
):
    wm_copy, wa_copy, wo_copy, x_copy = fetch(
        [(wm_hbm, wm_ref), (wa_hbm, wa_ref), (wo_hbm, wo_ref), (x_hbm, x_ref)], sems
    )
    n = x_ref.shape[0]
    hidden = silu(dot(far_ref[...], ws_ref[...]) + base_ref[...].astype(F32)).astype(BF16)
    scatter = one_hot_t([lr_ref[b : b + 1, :] for b in range(lr_ref.shape[0])], n)
    wm_copy.wait()
    message = normalize(dot(hidden, wm_ref[...])).astype(BF16)
    aggregate = (agg_ref[...] + dot(scatter, message)).astype(BF16)
    wa_copy.wait()
    node_hidden = silu(nself_ref[...].astype(F32) + dot(aggregate, wa_ref[...])).astype(BF16)
    wo_copy.wait()
    x_copy.wait()
    fresh = (x_ref[...].astype(F32) + dot(node_hidden, wo_ref[...])).astype(BF16)
    out_ref[...] = fresh
    first_ref[...] = fresh[:BORDER]
    last_ref[...] = fresh[n - BORDER :]


def own_kernel(
    off_ref, ds_ref, geo_ref, wdgeo_ref, x_ref, grid_hbm, wds_hbm, wdg_hbm, wgs_hbm, wf_hbm, wga_hbm,
    fresh_hbm, pre_ref, gproj_ref, gself_ref, wds_ref, wf_ref, wga_ref,
    tab, gsc, wsc, grid_ref, wdg_ref, wgs_ref, sems,
):
    wds_copy, wdg_copy, grid_copy, wgs_copy, wf_copy, wga_copy, fresh_copy = fetch(
        [
            (wds_hbm, wds_ref), (wdg_hbm, wdg_ref), (grid_hbm, grid_ref), (wgs_hbm, wgs_ref),
            (wf_hbm, wf_ref), (wga_hbm, wga_ref), (x_ref, fresh_hbm),
        ],
        sems,
    )
    n = x_ref.shape[0]
    vertices, points = ds_ref.shape
    features = geo_ref.shape[0] // vertices
    tab[n : n + LANES, :] = geo_table(wdgeo_ref, wsc)
    tab[n + LANES :, :] = jnp.zeros((LANES, tab.shape[1]), BF16)
    wds_copy.wait()
    tab[0:n, :] = dot(x_ref[...], wds_ref[...]).astype(BF16)
    wdg_copy.wait()
    grid_copy.wait()
    gproj_ref[...] = dot(grid_ref[...], wdg_ref[...])
    start = off_ref[0] + BORDER
    for v in range(vertices):
        gsc[...] = jnp.zeros(gsc.shape, F32)
        for c in range(features):
            high, low = split(geo_ref[c * vertices + v : c * vertices + v + 1, :])
            gsc[c : c + 1, :] = high
            gsc[8 + c : 9 + c, :] = low
            gsc[16 + c : 17 + c, :] = high
        send = columns([ds_ref[v : v + 1, b : b + LANES] - start for b in range(0, points, LANES)])
        empty = jnp.zeros((points, LANES), BF16)
        lhs = jnp.concatenate([one_hot(send, n), geo_columns(gsc[...]), empty], axis=1)
        pre_ref[v * points : (v + 1) * points, :] = dot(lhs, tab[...])
    wgs_copy.wait()
    gself_ref[...] = dot(grid_ref[...], wgs_ref[...])
    wf_copy.wait()
    wga_copy.wait()
    fresh_copy.wait()


def grid_kernel(
    off_ref, ds_ref, before_ref, after_ref, pre_ref, gproj_ref, gself_ref, wds_ref, wf_ref, wga_ref, wp_ref,
    out_ref, *, nodes,
):
    vertices, points = ds_ref.shape
    halo = jnp.concatenate(
        [dot(before_ref[...], wds_ref[...]), dot(after_ref[...], wds_ref[...])], axis=0
    ).astype(BF16)
    off = off_ref[0]
    total = jnp.zeros((points, gself_ref.shape[1]), F32)
    for v in range(vertices):
        rows = []
        for b in range(0, points, LANES):
            place = ds_ref[v : v + 1, b : b + LANES] - off
            rows.append(
                jnp.where(place < BORDER, place, jnp.where(place >= BORDER + nodes, place - nodes, -1))
            )
        lhs = one_hot(columns(rows), 2 * BORDER)
        hidden = silu(
            dot(lhs, halo) + (pre_ref[v * points : (v + 1) * points, :] + gproj_ref[...])
        ).astype(BF16)
        total = total + normalize(dot(hidden, wf_ref[...]))
    hidden = silu(dot(total.astype(BF16), wga_ref[...]) + gself_ref[...]).astype(BF16)
    out_ref[...] = lax.dot_general(
        wp_ref[...], hidden, (((1,), (1,)), ((), ())), preferred_element_type=F32
    ).astype(BF16)


VM = pl.BlockSpec(memory_space=pltpu.MemorySpace.VMEM)
SM = pl.BlockSpec(memory_space=pltpu.MemorySpace.SMEM)
AN = pl.BlockSpec(memory_space=pltpu.MemorySpace.HBM)


def call(kernel, outs, ins, out_specs, scratch=(), mib=24, flops=0):
    return pl.pallas_call(
        kernel,
        out_shape=outs,
        in_specs=ins,
        out_specs=out_specs,
        scratch_shapes=list(scratch),
        compiler_params=pltpu.CompilerParams(vmem_limit_bytes=mib << 20),
        cost_estimate=pl.CostEstimate(flops=flops, transcendentals=0, bytes_accessed=1 << 22),
    )


def far_memory(*arrays):
    return [pltpu.with_memory_space_constraint(a, pltpu.MemorySpace.HBM) for a in arrays]


def swap(first, last):
    size = lax.axis_size("region")
    up = [(i, i + 1) for i in range(size - 1)]
    down = [(j, i) for i, j in up]
    return lax.ppermute(last, "region", up), lax.ppermute(first, "region", down)


def body(
    node_latent, grid_latent, fine_edge_sender, short_recv, short_geo, long_send, long_recv,
    long_geo, dec_send, dec_geo, w_send, w_recv, w_edge_geo, w_message, w_node_self, w_node_agg,
    w_node_out, w_dec_send, w_dec_grid, w_dec_geo, decoding_link_final_matrix, w_grid_agg,
    w_grid_self, final_projection_matrix,
):
    n, h = node_latent.shape
    points = grid_latent.shape[0]
    edges = fine_edge_sender.shape[0]
    far = long_send.shape[0]
    vertices = dec_send.shape[0]
    outputs = final_projection_matrix.shape[0]
    regions = lax.axis_size("region")
    slot = far // regions
    rings = regions // BLOCK
    offset = (lax.axis_index("region") * n - BORDER).astype(jnp.int32).reshape(1)

    classes = [[q + BLOCK * i for i in range(rings)] for q in range(BLOCK)]
    blocks = [[BLOCK * b + q for q in range(BLOCK)] for b in range(rings)]
    group = jnp.arange(regions, dtype=jnp.int32)
    wanted = jnp.maximum(long_send.reshape(regions, slot) - (group * n)[:, None], 0)
    wanted = (wanted + (group // BLOCK * COARSE)[:, None]).reshape(rings, BLOCK, slot)
    wanted = wanted.transpose(1, 0, 2).reshape(BLOCK, 1, rings * slot)
    wanted = jnp.broadcast_to(
        jnp.pad(wanted, ((0, 0), (0, 0), (0, LANES - rings * slot))), (BLOCK, 8, LANES)
    )
    asked = lax.all_to_all(
        wanted, "region", split_axis=0, concat_axis=0, tiled=True, axis_index_groups=blocks
    )
    table = lax.all_gather(
        node_latent[:COARSE], "region", axis=0, tiled=True, axis_index_groups=classes
    )
    whole = jax.ShapeDtypeStruct((n, h), BF16)
    field = jax.ShapeDtypeStruct((points, h), F32)
    weight = jax.ShapeDtypeStruct((h, h), BF16)
    rows = call(relay_kernel, jax.ShapeDtypeStruct((far, h), BF16), [VM, VM], VM, mib=8)(asked, table)
    rows, node_later = lax.optimization_barrier((rows, node_latent))
    fetched = lax.all_to_all(
        rows.reshape(BLOCK, far // BLOCK, h), "region",
        split_axis=0, concat_axis=0, tiled=True, axis_index_groups=blocks,
    ).reshape(far, h)

    target = jnp.where(long_send >= 0, long_recv, -1)
    target = target.reshape(rings, BLOCK, slot).transpose(1, 0, 2).reshape(far // LANES, LANES)
    far_geo = long_geo.reshape(-1, rings, BLOCK, slot).transpose(0, 2, 1, 3).reshape(-1, far)
    before, after = swap(node_latent[:BORDER], node_latent[n - BORDER :])
    tile = 512
    ext = n + 2 * BORDER
    dense = pltpu.VMEM((h, h), BF16)
    aggregate, base, node_self, send_weight = call(
        functools.partial(fine_kernel, tile=tile),
        (jax.ShapeDtypeStruct((n, h), F32), jax.ShapeDtypeStruct((far, h), BF16), whole, weight),
        [SM] + [VM] * 8 + [AN] * 5,
        (VM,) * 4,
        [
            pltpu.VMEM((ext + n + LANES, h), BF16),
            pltpu.VMEM((edges, h), BF16),
            pltpu.VMEM((32, edges), F32),
            pltpu.VMEM((32, far), F32),
            pltpu.VMEM((32, h), F32),
            pltpu.VMEM((n, h), BF16),
            dense, dense, dense,
            pltpu.SemaphoreType.DMA((5,)),
        ],
        mib=28,
        flops=8 * edges * h * h,
    )(
        offset, fine_edge_sender.reshape(-1, LANES), short_recv.reshape(-1, LANES), short_geo,
        target, far_geo, before, after, w_edge_geo,
        *far_memory(node_later, w_send, w_recv, w_message, w_node_self),
    )
    border = jax.ShapeDtypeStruct((BORDER, h), BF16)
    fresh, first, last = call(
        node_kernel,
        (whole, border, border),
        [VM] * 6 + [AN] * 4,
        (VM,) * 3,
        [pltpu.VMEM((n, h), BF16), dense, dense, dense, pltpu.SemaphoreType.DMA((4,))],
        mib=16,
        flops=10 * n * h * h,
    )(
        target, fetched, aggregate, base, node_self, send_weight,
        *far_memory(node_later, w_message, w_node_agg, w_node_out),
    )
    before, after = swap(first, last)
    refreshed, pre, grid_proj, grid_self, dec_weight, final_weight, agg_weight = call(
        own_kernel,
        (
            whole, jax.ShapeDtypeStruct((vertices * points, h), F32),
            field, field, weight, weight, weight,
        ),
        [SM] + [VM] * 4 + [AN] * 6,
        (AN,) + (VM,) * 6,
        [
            pltpu.VMEM((n + 2 * LANES, h), BF16),
            pltpu.VMEM((32, points), F32),
            pltpu.VMEM((32, h), F32),
            pltpu.VMEM((points, h), BF16),
            dense, dense,
            pltpu.SemaphoreType.DMA((7,)),
        ],
        mib=20,
        flops=10 * n * h * h,
    )(
        offset, dec_send, dec_geo.reshape(-1, points), w_dec_geo, fresh,
        *far_memory(
            grid_latent, w_dec_send, w_dec_grid, w_grid_self, decoding_link_final_matrix, w_grid_agg
        ),
    )
    predicted = call(
        functools.partial(grid_kernel, nodes=n),
        jax.ShapeDtypeStruct((outputs, points), BF16),
        [SM] + [VM] * 10,
        VM,
        mib=20,
        flops=12 * n * h * h,
    )(
        offset, dec_send, before, after, pre, grid_proj, grid_self, dec_weight, final_weight, agg_weight,
        final_projection_matrix,
    )
    return (refreshed, predicted)


def solution(mesh):
    rows = P(("ens", "region"), None)
    line = P(("ens", "region"))
    in_specs = (
        rows, rows, line, line, P(None, ("ens", "region")), line, line, P(None, ("ens", "region")),
        P(None, ("ens", "region")), P(None, None, ("ens", "region")),
    ) + (P(),) * 14
    out_specs = (rows, P(None, ("ens", "region")))
    return jax.shard_map(body, mesh=mesh, in_specs=in_specs, out_specs=out_specs, check_vma=False)
```

time: 195 us -> 115 us (0.59)
  matrix products: 40.7 us -> 0 us
  blocking collectives: 0 us -> 38.7 us
  local copies, waits for them, and re-layouts: 37.2 us -> 2.9 us
  other arithmetic: 25.5 us -> 0.09 us
  waiting for transfers between devices: 27.4 us -> 5.2 us
  Pallas kernels: 0 us -> 22.1 us
  starting transfers between devices: 62.5 us -> 44.3 us
    dot_general x19 -> x0, matrix products: 40.7 us -> none  [the longest x13 23.5 us: product(): return jnp.dot(left, right, preferred_element_type=jnp.float32)]
    all_gather x0 -> x1, blocking collectives: none -> 38.7 us  [body(): lax.all_gather(node_latent[:COARSE], 'region', axis=0, tiled=True, axis_i...]
    gather x7 -> x0, local copies, waits for them, and re-layouts: 28.4 us -> none  [the longest x1 8.99 us: body(): send_ext[fine_edge_sender - row_offset] + recv_proj[short_recv]]
    all_to_all x2, waiting for transfers between devices: 23.8 us -> 0.01 us  [the longest x1 0.01 us: body(): lax.all_to_all(rows.reshape(BLOCK, far // BLOCK, h), 'region', split_axis...]
    pallas_call x0 -> x5, Pallas kernels: none -> 22.1 us  [the longest x1 10 us: body(): call(functools.partial(fine_kernel, tile=tile), (jax.ShapeDtypeStruct((n,...]
    scatter-add x2 -> x0, other arithmetic: 17.7 us -> none  [body(): aggregate = jnp.zeros((node_count, channel_count), jnp.float32).at[short_...]
    ppermute x4, starting transfers between devices: 29.2 us -> 12.3 us  [the longest x2 8.23 us: swap(): lax.ppermute(last, 'region', up)]
    mul x2 -> x0, local copies, waits for them, and re-layouts: 6.91 us -> none  [the longest x1 5.36 us: normalize(): return middle_point * lax.rsqrt(spread + 1e-05)]
  transfers between devices with their start and end apart: 6 -> 6, of which waited for: 3 -> 2; matrix products, arithmetic and copies ran while one was open for 34% -> 1% of each run, Pallas kernels for 0% -> 12%
where the time goes in v1:
time: 115 us; the launch traced here: 114 us
  starting transfers between devices  44.3 us (39%)
  blocking collectives  38.7 us (34%)
  Pallas kernels  22.1 us (19%)
  waiting for transfers between devices  5.2 us (5%)
  local copies, waits for them, and re-layouts  2.9 us (3%)
    all_gather x1, blocking collectives, body(): lax.all_gather(node_latent[:COARSE], 'region', axis=0, tiled=True, axis_i...  38.7 us
    all_to_all x1, starting transfers between devices, body(): lax.all_to_all(wanted, 'region', split_axis=0, concat_axis=0, tiled=True,...  23.7 us
    pallas_call x1, Pallas kernels, body(): call(functools.partial(fine_kernel, tile=tile), (jax.ShapeDtypeStruct((n,...  10 us
    all_to_all x1, starting transfers between devices, body(): lax.all_to_all(rows.reshape(BLOCK, far // BLOCK, h), 'region', split_axis...  8.37 us
    ppermute x2, starting transfers between devices, swap(): lax.ppermute(last, 'region', up)  8.23 us
    ppermute x2, starting transfers between devices, swap(): lax.ppermute(first, 'region', down)  4.07 us
    pallas_call x1, Pallas kernels, body(): call(functools.partial(grid_kernel, nodes=n), jax.ShapeDtypeStruct((outpu...  3.86 us
    pallas_call x1, Pallas kernels, body(): call(own_kernel, (whole, jax.ShapeDtypeStruct((vertices * points, h), F32...  3.86 us
  transfers between devices with their start and end apart: 6, of which 2 were waited for; matrix products, arithmetic and copies ran while one was open for 1% of the time, Pallas kernels for 12%

profile of v1, /device:TPU:37, one launch (start us, length us, event | category | flops | bytes accessed | tf_op | source)
XLA Modules:
  0.0 114.3 jit_solution(5772366982565363106)
XLA Ops:
  0.6 0.0 copy-start.9
  0.7 0.8 reshape.76
  1.5 0.1 add_bitcast_fusion
  1.6 0.1 reshape.77
  1.7 0.6 broadcast_in_dim.15
  2.3 23.7 %all-to-all-start = ((s32[8,8,128]{2,1,0:T(8,128)}), s32[8,8,128]{2,1,0:T(8,128)S(1)}, u32[]{:S(2)}, u32[]{:S(2)}) async-start(s32[8,8,128]{2,1,0:T(8,128)} %broadcast_in_dim.15), calls=%async_computation | async-start | bytes 65536 | tf_op jit(solution)/shard_map/all_to_all | solution.py:295
  26.0 0.9 fusion.3
  26.9 38.7 %all_gather.3.table_ref = bf16[512,512]{1,0:T(8,128)(2,1)S(1)} all-gather(bf16[64,512]{1,0:T(8,128)(2,1)S(1)} %get-tuple-element.35), channel_id=1, replica_groups={{0,8,16,24,32,40,48,56},{1,9,17,25,33,41,49,57},{2,10,18,26,34,42,50,58..., dimensions={0}, use_global_device_ids=true | all-gather | bytes 589824 | tf_op jit(solution)/shard_map/all_gather | solution.py:298
  65.6 1.3 %shard_map.239 = bf16[512,512]{1,0:T(8,128)(2,1)} custom-call(s32[8,8,128]{2,1,0:T(8,128)S(1)} %all-to-all-done.asked_ref, bf16[512,512]{1,0:T(8,128)(2,1)S(1)} %all_gather.3.table_ref), custom_call_target="tpu_custom_call" | custom-call | bytes 4194304 | tf_op jit(solution)/shard_map/pallas_call | solution.py:304
  66.9 8.4 %all-to-all-start.1 = ((bf16[8,64,512]{2,1,0:T(8,128)(2,1)}), bf16[8,64,512]{2,1,0:T(8,128)(2,1)S(1)}, u32[]{:S(2)}, u32[]{:S(2)}) async-start(bf16[8,64,512]{2,1,0:T(8,128)(2,1)} %bitcast.4), calls=%async_computation.1 | async-start | bytes 1048576 | tf_op jit(solution)/shard_map/all_to_all | solution.py:306
  75.3 1.9 %collective-permute-start.1 = (bf16[64,512]{1,0:T(8,128)(2,1)S(1)}, bf16[64,512]{1,0:T(8,128)(2,1)S(1)}, u32[]{:S(2)}, u32[]{:S(2)}) collective-permute-start(bf16[64,512]{1,0:T(8,128)(2,1)S(1)} %get-tuple-element.35), channel_id=1, source_target_pairs={{1,0},{2,1},{3,2},{4,3},{5,4},{6,5},{7,6},{8,7},{9,8},{10,9},{11,1... | collective-permute-start | bytes 196616 | tf_op jit(solution)/shard_map/ppermute | solution.py:266
  77.2 3.7 %collective-permute-start = (bf16[64,512]{1,0:T(8,128)(2,1)S(1)}, bf16[64,512]{1,0:T(8,128)(2,1)S(1)}, u32[]{:S(2)}, u32[]{:S(2)}) collective-permute-start(bf16[64,512]{1,0:T(8,128)(2,1)S(1)} %get-tuple-element.34), channel_id=1, source_target_pairs={{0,1},{1,2},{2,3},{3,4},{4,5},{5,6},{6,7},{7,8},{8,9},{9,10},{10,1... | collective-permute-start | bytes 196616 | tf_op jit(solution)/shard_map/ppermute | solution.py:266
  80.9 0.1 reshape.74
  81.0 0.1 reshape.75.lr_ref
  81.2 0.1 reshape.82
  81.3 0.1 reshape.83.lgeo_ref
  81.4 3.7 %collective-permute-done.before_ref = bf16[64,512]{1,0:T(8,128)(2,1)S(1)} collective-permute-done((bf16[64,512]{1,0:T(8,128)(2,1)S(1)}, bf16[64,512]{1,0:T(8,128)(2,1)S(1)}, u32[]{:S(2)}, u32[]{:S(2)}) %collective-permute-start) | collective-permute-done | bytes 65568 | tf_op jit(solution)/shard_map/ppermute | solution.py:266
  85.1 10.0 %shard_map.240 = (f32[512,512]{1,0:T(8,128)S(1)}, bf16[512,512]{1,0:T(8,128)(2,1)S(1)}, bf16[512,512]{1,0:T(8,128)(2,1)S(1)}, bf16[512,512]{1,0:T(8,128)(2,1)S(1)}) custom-call(s32[1]{0:T(128)} %bitcast.off_ref, s32[16,128]{1,0:T(8,128)S(1)} %bitcast.16, s32[16,128]{1,0:T(8,128)S(1)} %bitcast.17, f32[4,2048]{1,0:T(4,128)S(1)} %copy-done.2, ...), custom_call_target="tpu_custom_call" | custom-call | flops 4294967296 | bytes 4194304 | tf_op jit(solution)/shard_map/pallas_call | solution.py:318
  95.2 3.1 %shard_map.241 = (bf16[512,512]{1,0:T(8,128)(2,1)S(1)}, bf16[64,512]{1,0:T(8,128)(2,1)S(1)}, bf16[64,512]{1,0:T(8,128)(2,1)S(1)}) custom-call(s32[4,128]{1,0:T(4,128)S(1)} %reshape.75.lr_ref, bf16[512,512]{1,0:T(8,128)(2,1)S(1)} %bitcast.15, f32[512,512]{1,0:T(8,128)S(1)} %get-tuple-element.20.agg_ref, bf16[512,512]{1,0:T(8,128)(2,1)S(1)} %get-tuple-element.21.base_ref, ...), custom_call_target="tpu_custom_call" | custom-call | flops 1342177280 | bytes 4194304 | tf_op jit(solution)/shard_map/pallas_call | solution.py:341
  98.3 4.6 %collective-permute-start.2 = (bf16[64,512]{1,0:T(8,128)(2,1)S(1)}, bf16[64,512]{1,0:T(8,128)(2,1)S(1)}, u32[]{:S(2)}, u32[]{:S(2)}) collective-permute-start(bf16[64,512]{1,0:T(8,128)(2,1)S(1)} %get-tuple-element.26), channel_id=1, source_target_pairs={{0,1},{1,2},{2,3},{3,4},{4,5},{5,6},{6,7},{7,8},{8,9},{9,10},{10,1... | collective-permute-start | bytes 196616 | tf_op jit(solution)/shard_map/ppermute | solution.py:266
  102.9 2.1 %collective-permute-start.3 = (bf16[64,512]{1,0:T(8,128)(2,1)S(1)}, bf16[64,512]{1,0:T(8,128)(2,1)S(1)}, u32[]{:S(2)}, u32[]{:S(2)}) collective-permute-start(bf16[64,512]{1,0:T(8,128)(2,1)S(1)} %get-tuple-element.27), channel_id=1, source_target_pairs={{1,0},{2,1},{3,2},{4,3},{5,4},{6,5},{7,6},{8,7},{9,8},{10,9},{11,1... | collective-permute-start | bytes 196616 | tf_op jit(solution)/shard_map/ppermute | solution.py:266
  105.0 3.9 %shard_map.242 = (bf16[512,512]{1,0:T(8,128)(2,1)}, f32[1536,512]{1,0:T(8,128)S(1)}, f32[512,512]{1,0:T(8,128)S(1)}, f32[512,512]{1,0:T(8,128)S(1)}, bf16[512,51...) custom-call(s32[1]{0:T(128)} %bitcast.off_ref, s32[3,512]{1,0:T(4,128)S(1)} %copy-done.1, ...), custom_call_target="tpu_custom_call" | custom-call | flops 1342177280 | bytes 4194304 | tf_op jit(solution)/shard_map/pallas_call | solution.py:354
  108.9 1.5 %collective-permute-done.3.after_ref = bf16[64,512]{1,0:T(8,128)(2,1)S(1)} collective-permute-done((bf16[64,512]{1,0:T(8,128)(2,1)S(1)}, bf16[64,512]{1,0:T(8,128)(2,1)S(1)}, u32[]{:S(2)}, u32[]{:S(2)}) %collective-permute-start.3) | collective-permute-done | bytes 65568 | tf_op jit(solution)/shard_map/ppermute | solution.py:266
  110.5 3.9 %shard_map.243 = bf16[100,512]{1,0:T(8,128)(2,1)} custom-call(s32[1]{0:T(128)} %bitcast.off_ref, s32[3,512]{1,0:T(4,128)S(1)} %copy-done.1, bf16[64,512]{1,0:T(8,128)(2,1)S(1)} %collective-permute-done.2.before_ref, bf16[64,512]{1,0:T(8,128)(2,1)S(1)} %collective-permute-done.3.after_ref, f32[1536,512]{1,0:T(8,128)S(1)} %get-tuple-element.28.pre_ref, ...), custom_call_target="tpu_custom_call" | custom-call | flops 1610612736 | bytes 4194304 | tf_op jit(solution)/shard_map/pallas_call | solution.py:378
  (33 shorter events, 0.2 us)
Async XLA Ops:
  0.6 80.3 %copy-start.9 = (s32[512]{0:T(512)S(1)}, s32[512]{0:T(512)}, u32[]{:S(2)}) copy-start(s32[512]{0:T(512)} %param.29) | copy-start | bytes 6148
  0.6 80.2 %copy-start.10 = (s32[512]{0:T(512)S(1)}, s32[512]{0:T(512)}, u32[]{:S(2)}) copy-start(s32[512]{0:T(512)} %param.30) | copy-start | bytes 6148
  0.7 80.5 %copy-start.7 = (f32[4,3,512]{2,0,1:T(4,128)S(1)}, f32[4,3,512]{2,0,1:T(4,128)}, u32[]{:S(2)}) copy-start(f32[4,3,512]{2,0,1:T(4,128)} %param.33) | copy-start | bytes 73732
  0.7 80.5 %copy-start.8 = (f32[4,512]{1,0:T(4,128)S(1)}, f32[4,512]{1,0:T(4,128)}, u32[]{:S(2)}) copy-start(f32[4,512]{1,0:T(4,128)} %param.31) | copy-start | bytes 24580
  0.7 84.4 %copy-start.5 = (f32[4,512]{1,0:T(4,128)S(1)}, f32[4,512]{1,0:T(4,128)}, u32[]{:S(2)}) copy-start(f32[4,512]{1,0:T(4,128)} %weg_ref.1) | copy-start | bytes 24580
  0.7 84.4 %copy-start.2 = (f32[4,2048]{1,0:T(4,128)S(1)}, f32[4,2048]{1,0:T(4,128)}, u32[]{:S(2)}) copy-start(f32[4,2048]{1,0:T(4,128)} %geo_ref.1) | copy-start | bytes 98308
  0.7 84.4 %copy-start.4 = (s32[2048]{0:T(1024)S(1)}, s32[2048]{0:T(1024)}, u32[]{:S(2)}) copy-start(s32[2048]{0:T(1024)} %param.27) | copy-start | bytes 24580
  0.7 84.4 %copy-start.3 = (s32[2048]{0:T(1024)S(1)}, s32[2048]{0:T(1024)}, u32[]{:S(2)}) copy-start(s32[2048]{0:T(1024)} %param.26) | copy-start | bytes 24580
  2.3 63.3 %all-to-all-start = ((s32[8,8,128]{2,1,0:T(8,128)}), s32[8,8,128]{2,1,0:T(8,128)S(1)}, u32[]{:S(2)}, u32[]{:S(2)}) async-start(s32[8,8,128]{2,1,0:T(8,128)} %broadcast_in_dim.15), calls=%async_computation | async-start | bytes 65536 | tf_op jit(solution)/shard_map/all_to_all | solution.py:295
  66.9 28.3 %all-to-all-start.1 = ((bf16[8,64,512]{2,1,0:T(8,128)(2,1)}), bf16[8,64,512]{2,1,0:T(8,128)(2,1)S(1)}, u32[]{:S(2)}, u32[]{:S(2)}) async-start(bf16[8,64,512]{2,1,0:T(8,128)(2,1)} %bitcast.4), calls=%async_computation.1 | async-start | bytes 1048576 | tf_op jit(solution)/shard_map/all_to_all | solution.py:306
  75.3 9.8 %collective-permute-start.1 = (bf16[64,512]{1,0:T(8,128)(2,1)S(1)}, bf16[64,512]{1,0:T(8,128)(2,1)S(1)}, u32[]{:S(2)}, u32[]{:S(2)}) collective-permute-start(bf16[64,512]{1,0:T(8,128)(2,1)S(1)} %get-tuple-element.35), channel_id=1, source_target_pairs={{1,0},{2,1},{3,2},{4,3},{5,4},{6,5},{7,6},{8,7},{9,8},{10,9},{11,1... | collective-permute-start | bytes 196616 | tf_op jit(solution)/shard_map/ppermute | solution.py:266
  77.2 7.9 %collective-permute-start = (bf16[64,512]{1,0:T(8,128)(2,1)S(1)}, bf16[64,512]{1,0:T(8,128)(2,1)S(1)}, u32[]{:S(2)}, u32[]{:S(2)}) collective-permute-start(bf16[64,512]{1,0:T(8,128)(2,1)S(1)} %get-tuple-element.34), channel_id=1, source_target_pairs={{0,1},{1,2},{2,3},{3,4},{4,5},{5,6},{6,7},{7,8},{8,9},{9,10},{10,1... | collective-permute-start | bytes 196616 | tf_op jit(solution)/shard_map/ppermute | solution.py:266
  95.2 9.8 %copy-start.1 = (s32[3,512]{1,0:T(4,128)S(1)}, s32[3,512]{1,0:T(4,128)}, u32[]{:S(2)}) copy-start(s32[3,512]{1,0:T(4,128)} %ds_ref.3) | copy-start | bytes 18436
  95.2 9.8 %copy-start.6 = (f32[4,512]{1,0:T(4,128)S(1)}, f32[4,512]{1,0:T(4,128)}, u32[]{:S(2)}) copy-start(f32[4,512]{1,0:T(4,128)} %wdgeo_ref.1) | copy-start | bytes 24580
  98.3 12.2 %copy-start = (bf16[100,512]{1,0:T(8,128)(2,1)S(1)}, bf16[100,512]{1,0:T(8,128)(2,1)}, u32[]{:S(2)}) copy-start(bf16[100,512]{1,0:T(8,128)(2,1)} %wp_ref.1) | copy-start | bytes 307204
  98.3 10.6 %collective-permute-start.2 = (bf16[64,512]{1,0:T(8,128)(2,1)S(1)}, bf16[64,512]{1,0:T(8,128)(2,1)S(1)}, u32[]{:S(2)}, u32[]{:S(2)}) collective-permute-start(bf16[64,512]{1,0:T(8,128)(2,1)S(1)} %get-tuple-element.26), channel_id=1, source_target_pairs={{0,1},{1,2},{2,3},{3,4},{4,5},{5,6},{6,7},{7,8},{8,9},{9,10},{10,1... | collective-permute-start | bytes 196616 | tf_op jit(solution)/shard_map/ppermute | solution.py:266
  102.9 7.6 %collective-permute-start.3 = (bf16[64,512]{1,0:T(8,128)(2,1)S(1)}, bf16[64,512]{1,0:T(8,128)(2,1)S(1)}, u32[]{:S(2)}, u32[]{:S(2)}) collective-permute-start(bf16[64,512]{1,0:T(8,128)(2,1)S(1)} %get-tuple-element.27), channel_id=1, source_target_pairs={{1,0},{2,1},{3,2},{4,3},{5,4},{6,5},{7,6},{8,7},{9,8},{10,9},{11,1... | collective-permute-start | bytes 196616 | tf_op jit(solution)/shard_map/ppermute | solution.py:266

commit v2 on v1

--- a/solution.py
+++ b/solution.py
@@ -94,12 +94,15 @@
 
 def fine_kernel(
     off_ref, fs_ref, sr_ref, geo_ref, lr_ref, lgeo_ref, before_ref, after_ref, weg_ref,
-    x_hbm, ws_hbm, wr_hbm, wm_hbm, wself_hbm,
-    agg_ref, base_ref, nself_ref, ws_ref,
-    tab, msg, gsc, lsc, wsc, x_ref, wr_ref, wm_ref, wself_ref, sems, *, tile,
+    x_hbm, ws_hbm, wr_hbm, wm_hbm, wself_hbm, grid_hbm, wdg_hbm, wgs_hbm,
+    agg_ref, base_ref, nself_ref, ws_ref, gproj_ref, gself_ref,
+    tab, msg, gsc, lsc, wsc, x_ref, wr_ref, wm_ref, wself_ref, grid_ref, wdg_ref, wgs_ref, sems, *, tile,
 ):
-    x_copy, ws_copy, wr_copy, wm_copy, wself_copy = fetch(
-        [(x_hbm, x_ref), (ws_hbm, ws_ref), (wr_hbm, wr_ref), (wm_hbm, wm_ref), (wself_hbm, wself_ref)],
+    x_copy, ws_copy, wr_copy, wm_copy, wself_copy, grid_copy, wdg_copy, wgs_copy = fetch(
+        [
+            (x_hbm, x_ref), (ws_hbm, ws_ref), (wr_hbm, wr_ref), (wm_hbm, wm_ref),
+            (wself_hbm, wself_ref), (grid_hbm, grid_ref), (wdg_hbm, wdg_ref), (wgs_hbm, wgs_ref),
+        ],
         sems,
     )
     n, h = x_ref.shape
@@ -120,6 +123,11 @@
     tab[ext : ext + n, :] = dot(x, wr_ref[...]).astype(BF16)
     wself_copy.wait()
     nself_ref[...] = dot(x, wself_ref[...]).astype(BF16)
+    grid_copy.wait()
+    wdg_copy.wait()
+    gproj_ref[...] = dot(grid_ref[...], wdg_ref[...]).astype(BF16)
+    wgs_copy.wait()
+    gself_ref[...] = dot(grid_ref[...], wgs_ref[...]).astype(BF16)
     wm_copy.wait()
     off = off_ref[0]
     per = tile // LANES
@@ -170,14 +178,14 @@
 
 
 def own_kernel(
-    off_ref, ds_ref, geo_ref, wdgeo_ref, x_ref, grid_hbm, wds_hbm, wdg_hbm, wgs_hbm, wf_hbm, wga_hbm,
-    fresh_hbm, pre_ref, gproj_ref, gself_ref, wds_ref, wf_ref, wga_ref,
-    tab, gsc, wsc, grid_ref, wdg_ref, wgs_ref, sems,
+    off_ref, ds_ref, geo_ref, wdgeo_ref, x_ref, wds_hbm, gproj_hbm, gself_hbm, wf_hbm, wga_hbm,
+    fresh_hbm, pre_ref, gself_ref, wds_ref, wf_ref, wga_ref,
+    tab, gsc, wsc, gproj_ref, sems,
 ):
-    wds_copy, wdg_copy, grid_copy, wgs_copy, wf_copy, wga_copy, fresh_copy = fetch(
+    wds_copy, gproj_copy, gself_copy, wf_copy, wga_copy, fresh_copy = fetch(
         [
-            (wds_hbm, wds_ref), (wdg_hbm, wdg_ref), (grid_hbm, grid_ref), (wgs_hbm, wgs_ref),
-            (wf_hbm, wf_ref), (wga_hbm, wga_ref), (x_ref, fresh_hbm),
+            (wds_hbm, wds_ref), (gproj_hbm, gproj_ref), (gself_hbm, gself_ref), (wf_hbm, wf_ref),
+            (wga_hbm, wga_ref), (x_ref, fresh_hbm),
         ],
         sems,
     )
@@ -188,9 +196,7 @@
     tab[n + LANES :, :] = jnp.zeros((LANES, tab.shape[1]), BF16)
     wds_copy.wait()
     tab[0:n, :] = dot(x_ref[...], wds_ref[...]).astype(BF16)
-    wdg_copy.wait()
-    grid_copy.wait()
-    gproj_ref[...] = dot(grid_ref[...], wdg_ref[...])
+    gproj_copy.wait()
     start = off_ref[0] + BORDER
     for v in range(vertices):
         gsc[...] = jnp.zeros(gsc.shape, F32)
@@ -202,16 +208,15 @@
         send = columns([ds_ref[v : v + 1, b : b + LANES] - start for b in range(0, points, LANES)])
         empty = jnp.zeros((points, LANES), BF16)
         lhs = jnp.concatenate([one_hot(send, n), geo_columns(gsc[...]), empty], axis=1)
-        pre_ref[v * points : (v + 1) * points, :] = dot(lhs, tab[...])
-    wgs_copy.wait()
-    gself_ref[...] = dot(grid_ref[...], wgs_ref[...])
+        pre_ref[v * points : (v + 1) * points, :] = dot(lhs, tab[...]) + gproj_ref[...].astype(F32)
+    gself_copy.wait()
     wf_copy.wait()
     wga_copy.wait()
     fresh_copy.wait()
 
 
 def grid_kernel(
-    off_ref, ds_ref, before_ref, after_ref, pre_ref, gproj_ref, gself_ref, wds_ref, wf_ref, wga_ref, wp_ref,
+    off_ref, ds_ref, before_ref, after_ref, pre_ref, gself_ref, wds_ref, wf_ref, wga_ref, wp_ref,
     out_ref, *, nodes,
 ):
     vertices, points = ds_ref.shape
@@ -228,11 +233,9 @@
                 jnp.where(place < BORDER, place, jnp.where(place >= BORDER + nodes, place - nodes, -1))
             )
         lhs = one_hot(columns(rows), 2 * BORDER)
-        hidden = silu(
-            dot(lhs, halo) + (pre_ref[v * points : (v + 1) * points, :] + gproj_ref[...])
-        ).astype(BF16)
+        hidden = silu(dot(lhs, halo) + pre_ref[v * points : (v + 1) * points, :]).astype(BF16)
         total = total + normalize(dot(hidden, wf_ref[...]))
-    hidden = silu(dot(total.astype(BF16), wga_ref[...]) + gself_ref[...]).astype(BF16)
+    hidden = silu(dot(total.astype(BF16), wga_ref[...]) + gself_ref[...].astype(F32)).astype(BF16)
     out_ref[...] = lax.dot_general(
         wp_ref[...], hidden, (((1,), (1,)), ((), ())), preferred_element_type=F32
     ).astype(BF16)
@@ -295,11 +298,10 @@
     asked = lax.all_to_all(
         wanted, "region", split_axis=0, concat_axis=0, tiled=True, axis_index_groups=blocks
     )
-    table = lax.all_gather(
-        node_latent[:COARSE], "region", axis=0, tiled=True, axis_index_groups=classes
-    )
+    before, after = swap(node_latent[:BORDER], node_latent[n - BORDER :])
+    head, before, after = lax.optimization_barrier((node_latent[:COARSE], before, after))
+    table = lax.all_gather(head, "region", axis=0, tiled=True, axis_index_groups=classes)
     whole = jax.ShapeDtypeStruct((n, h), BF16)
-    field = jax.ShapeDtypeStruct((points, h), F32)
     weight = jax.ShapeDtypeStruct((h, h), BF16)
     rows = call(relay_kernel, jax.ShapeDtypeStruct((far, h), BF16), [VM, VM], VM, mib=8)(asked, table)
     rows, node_later = lax.optimization_barrier((rows, node_latent))
@@ -311,15 +313,15 @@
     target = jnp.where(long_send >= 0, long_recv, -1)
     target = target.reshape(rings, BLOCK, slot).transpose(1, 0, 2).reshape(far // LANES, LANES)
     far_geo = long_geo.reshape(-1, rings, BLOCK, slot).transpose(0, 2, 1, 3).reshape(-1, far)
-    before, after = swap(node_latent[:BORDER], node_latent[n - BORDER :])
     tile = 512
     ext = n + 2 * BORDER
     dense = pltpu.VMEM((h, h), BF16)
-    aggregate, base, node_self, send_weight = call(
+    field = jax.ShapeDtypeStruct((points, h), BF16)
+    aggregate, base, node_self, send_weight, grid_proj, grid_self = call(
         functools.partial(fine_kernel, tile=tile),
-        (jax.ShapeDtypeStruct((n, h), F32), jax.ShapeDtypeStruct((far, h), BF16), whole, weight),
-        [SM] + [VM] * 8 + [AN] * 5,
-        (VM,) * 4,
+        (jax.ShapeDtypeStruct((n, h), F32), jax.ShapeDtypeStruct((far, h), BF16), whole, weight, field, field),
+        [SM] + [VM] * 8 + [AN] * 8,
+        (VM,) * 6,
         [
             pltpu.VMEM((ext + n + LANES, h), BF16),
             pltpu.VMEM((edges, h), BF16),
@@ -328,14 +330,18 @@
             pltpu.VMEM((32, h), F32),
             pltpu.VMEM((n, h), BF16),
             dense, dense, dense,
-            pltpu.SemaphoreType.DMA((5,)),
+            pltpu.VMEM((points, h), BF16),
+            dense, dense,
+            pltpu.SemaphoreType.DMA((8,)),
         ],
         mib=28,
         flops=8 * edges * h * h,
     )(
         offset, fine_edge_sender.reshape(-1, LANES), short_recv.reshape(-1, LANES), short_geo,
         target, far_geo, before, after, w_edge_geo,
-        *far_memory(node_later, w_send, w_recv, w_message, w_node_self),
+        *far_memory(
+            node_later, w_send, w_recv, w_message, w_node_self, grid_latent, w_dec_grid, w_grid_self
+        ),
     )
     border = jax.ShapeDtypeStruct((BORDER, h), BF16)
     fresh, first, last = call(
@@ -351,39 +357,38 @@
         *far_memory(node_later, w_message, w_node_agg, w_node_out),
     )
     before, after = swap(first, last)
-    refreshed, pre, grid_proj, grid_self, dec_weight, final_weight, agg_weight = call(
+    refreshed, pre, grid_self, dec_weight, final_weight, agg_weight = call(
         own_kernel,
         (
             whole, jax.ShapeDtypeStruct((vertices * points, h), F32),
-            field, field, weight, weight, weight,
+            field, weight, weight, weight,
         ),
-        [SM] + [VM] * 4 + [AN] * 6,
-        (AN,) + (VM,) * 6,
+        [SM] + [VM] * 4 + [AN] * 5,
+        (AN,) + (VM,) * 5,
         [
             pltpu.VMEM((n + 2 * LANES, h), BF16),
             pltpu.VMEM((32, points), F32),
             pltpu.VMEM((32, h), F32),
             pltpu.VMEM((points, h), BF16),
-            dense, dense,
-            pltpu.SemaphoreType.DMA((7,)),
+            pltpu.SemaphoreType.DMA((6,)),
         ],
         mib=20,
         flops=10 * n * h * h,
     )(
         offset, dec_send, dec_geo.reshape(-1, points), w_dec_geo, fresh,
         *far_memory(
-            grid_latent, w_dec_send, w_dec_grid, w_grid_self, decoding_link_final_matrix, w_grid_agg
+            w_dec_send, grid_proj, grid_self, decoding_link_final_matrix, w_grid_agg
         ),
     )
     predicted = call(
         functools.partial(grid_kernel, nodes=n),
         jax.ShapeDtypeStruct((outputs, points), BF16),
-        [SM] + [VM] * 10,
+        [SM] + [VM] * 9,
         VM,
         mib=20,
         flops=12 * n * h * h,
     )(
-        offset, dec_send, before, after, pre, grid_proj, grid_self, dec_weight, final_weight, agg_weight,
+        offset, dec_send, before, after, pre, grid_self, dec_weight, final_weight, agg_weight,
         final_projection_matrix,
     )
     return (refreshed, predicted)

time: 115 us -> 111 us (0.965)
  waiting for transfers between devices: 5.2 us -> 1.39 us
  starting transfers between devices: 44.3 us -> 40.6 us
  blocking collectives: 38.7 us -> 41.3 us
  local copies, waits for them, and re-layouts: 2.9 us -> 4.51 us
    all_to_all x1, starting transfers between devices: 23.7 us -> 3.42 us  [body(): lax.all_to_all(wanted, 'region', split_axis=0, concat_axis=0, tiled=True,...]
    ppermute x2, starting transfers between devices: 4.07 us -> 20.8 us  [swap(): lax.ppermute(first, 'region', down)]
    ppermute x2, waiting for transfers between devices: 3.66 us -> 0.01 us  [swap(): lax.ppermute(last, 'region', up)]
    all_gather x1, blocking collectives: 38.7 us -> 41.3 us  [body(): lax.all_gather(head, 'region', axis=0, tiled=True, axis_index_groups=clas...]
    unnamed x23 -> x27, local copies, waits for them, and re-layouts: 0.07 us -> 1.66 us
    ppermute x2, waiting for transfers between devices: 1.54 us -> 0.17 us  [swap(): lax.ppermute(first, 'region', down)]
    all_to_all x1, waiting for transfers between devices: 0.01 us -> 1.21 us  [body(): lax.all_to_all(rows.reshape(BLOCK, far // BLOCK, h), 'region', split_axis...]
  transfers between devices with their start and end apart: 6 -> 6, of which waited for: 2 -> 2; matrix products, arithmetic and copies ran while one was open for 1% -> 2% of each run, Pallas kernels for 12% -> 13%
where the time goes in v2:
time: 111 us
  blocking collectives  41.3 us (37%)
  starting transfers between devices  40.6 us (37%)
  Pallas kernels  22.2 us (20%)
  local copies, waits for them, and re-layouts  4.51 us (4%)
  waiting for transfers between devices  1.39 us (1%)
    all_gather x1, blocking collectives, body(): lax.all_gather(head, 'region', axis=0, tiled=True, axis_index_groups=clas...  41.3 us
    ppermute x2, starting transfers between devices, swap(): lax.ppermute(first, 'region', down)  20.8 us
    pallas_call x1, Pallas kernels, body(): call(functools.partial(fine_kernel, tile=tile), (jax.ShapeDtypeStruct((n,...  10.9 us
    all_to_all x1, starting transfers between devices, body(): lax.all_to_all(rows.reshape(BLOCK, far // BLOCK, h), 'region', split_axis...  8.77 us
    ppermute x2, starting transfers between devices, swap(): lax.ppermute(last, 'region', up)  7.59 us
    pallas_call x1, Pallas kernels, body(): call(functools.partial(grid_kernel, nodes=n), jax.ShapeDtypeStruct((outpu...  3.71 us
    all_to_all x1, starting transfers between devices, body(): lax.all_to_all(wanted, 'region', split_axis=0, concat_axis=0, tiled=True,...  3.42 us
    pallas_call x1, Pallas kernels, body(): call(own_kernel, (whole, jax.ShapeDtypeStruct((vertices * points, h), F32...  3.2 us
  transfers between devices with their start and end apart: 6, of which 2 were waited for; matrix products, arithmetic and copies ran while one was open for 2% of the time, Pallas kernels for 13%

profile of v2, /device:TPU:37, one launch (start us, length us, event | category | flops | bytes accessed | tf_op | source)
XLA Modules:
  0.0 111.0 jit_solution(17350915988806022873)
XLA Ops:
  0.7 0.9 fusion.3
  1.6 5.1 %collective-permute-start = (bf16[64,512]{1,0:T(8,128)(2,1)S(1)}, bf16[64,512]{1,0:T(8,128)(2,1)S(1)}, u32[]{:S(2)}, u32[]{:S(2)}) collective-permute-start(bf16[64,512]{1,0:T(8,128)(2,1)S(1)} %get-tuple-element.42), channel_id=1, source_target_pairs={{0,1},{1,2},{2,3},{3,4},{4,5},{5,6},{6,7},{7,8},{8,9},{9,10},{10,1... | collective-permute-start | bytes 196616 | tf_op jit(solution)/shard_map/ppermute | solution.py:269
  6.7 18.6 %collective-permute-start.1 = (bf16[64,512]{1,0:T(8,128)(2,1)S(1)}, bf16[64,512]{1,0:T(8,128)(2,1)S(1)}, u32[]{:S(2)}, u32[]{:S(2)}) collective-permute-start(bf16[64,512]{1,0:T(8,128)(2,1)S(1)} %get-tuple-element.22), channel_id=1, source_target_pairs={{1,0},{2,1},{3,2},{4,3},{5,4},{6,5},{7,6},{8,7},{9,8},{10,9},{11,1... | collective-permute-start | bytes 196616 | tf_op jit(solution)/shard_map/ppermute | solution.py:269
  25.3 0.8 reshape.76
  26.1 0.1 add_bitcast_fusion
  26.3 0.6 broadcast_in_dim.15
  26.9 3.4 %all-to-all-start = ((s32[8,8,128]{2,1,0:T(8,128)}), s32[8,8,128]{2,1,0:T(8,128)S(1)}, u32[]{:S(2)}, u32[]{:S(2)}) async-start(s32[8,8,128]{2,1,0:T(8,128)} %broadcast_in_dim.15), calls=%async_computation | async-start | bytes 65536 | tf_op jit(solution)/shard_map/all_to_all | solution.py:298
  30.4 41.3 %all_gather.3.table_ref = bf16[512,512]{1,0:T(8,128)(2,1)S(1)} all-gather(bf16[64,512]{1,0:T(8,128)(2,1)S(1)} %get-tuple-element.22), channel_id=1, replica_groups={{0,8,16,24,32,40,48,56},{1,9,17,25,33,41,49,57},{2,10,18,26,34,42,50,58..., dimensions={0}, use_global_device_ids=true | all-gather | bytes 589824 | tf_op jit(solution)/shard_map/all_gather | solution.py:303
  71.6 1.3 %shard_map.239 = bf16[512,512]{1,0:T(8,128)(2,1)} custom-call(s32[8,8,128]{2,1,0:T(8,128)S(1)} %all-to-all-done.asked_ref, bf16[512,512]{1,0:T(8,128)(2,1)S(1)} %all_gather.3.table_ref), custom_call_target="tpu_custom_call" | custom-call | bytes 4194304 | tf_op jit(solution)/shard_map/pallas_call | solution.py:306
  72.9 8.8 %all-to-all-start.1 = ((bf16[8,64,512]{2,1,0:T(8,128)(2,1)}), bf16[8,64,512]{2,1,0:T(8,128)(2,1)S(1)}, u32[]{:S(2)}, u32[]{:S(2)}) async-start(bf16[8,64,512]{2,1,0:T(8,128)(2,1)} %bitcast.4), calls=%async_computation.1 | async-start | bytes 1048576 | tf_op jit(solution)/shard_map/all_to_all | solution.py:308
  81.7 0.1 reshape.74
  81.8 0.1 reshape.75.lr_ref
  82.0 0.1 reshape.82
  82.1 0.1 reshape.83.lgeo_ref
  82.3 10.9 %shard_map.240 = (f32[512,512]{1,0:T(8,128)S(1)}, bf16[512,512]{1,0:T(8,128)(2,1)S(1)}, bf16[512,512]{1,0:T(8,128)(2,1)S(1)}, bf16[512,512]{1,0:T(8,128)(2,1)S(1...) custom-call(s32[1]{0:T(128)} %bitcast.off_ref, s32[16,128]{1,0:T(8,128)S(1)} %bitcast.16, ...), custom_call_target="tpu_custom_call" | custom-call | flops 4294967296 | bytes 4194304 | tf_op jit(solution)/shard_map/pallas_call | solution.py:320
  93.2 0.8 copy-done.7
  94.0 0.8 copy-done.8
  94.8 1.2 %all-to-all-done.1 = bf16[8,64,512]{2,1,0:T(8,128)(2,1)S(1)} async-done(((bf16[8,64,512]{2,1,0:T(8,128)(2,1)}), bf16[8,64,512]{2,1,0:T(8,128)(2,1)S(1)}, u32[]{:S(2)}, u32[]{:S(2)}) %all-to-all-start.1) | async-done | bytes 524320 | tf_op jit(solution)/shard_map/all_to_all | solution.py:308
  96.1 3.1 %shard_map.241 = (bf16[512,512]{1,0:T(8,128)(2,1)S(1)}, bf16[64,512]{1,0:T(8,128)(2,1)S(1)}, bf16[64,512]{1,0:T(8,128)(2,1)S(1)}) custom-call(s32[4,128]{1,0:T(4,128)S(1)} %reshape.75.lr_ref, bf16[512,512]{1,0:T(8,128)(2,1)S(1)} %bitcast.15, f32[512,512]{1,0:T(8,128)S(1)} %get-tuple-element.27.agg_ref, bf16[512,512]{1,0:T(8,128)(2,1)S(1)} %get-tuple-element.28.base_ref, ...), custom_call_target="tpu_custom_call" | custom-call | flops 1342177280 | bytes 4194304 | tf_op jit(solution)/shard_map/pallas_call | solution.py:347
  99.2 2.5 %collective-permute-start.2 = (bf16[64,512]{1,0:T(8,128)(2,1)S(1)}, bf16[64,512]{1,0:T(8,128)(2,1)S(1)}, u32[]{:S(2)}, u32[]{:S(2)}) collective-permute-start(bf16[64,512]{1,0:T(8,128)(2,1)S(1)} %get-tuple-element.35), channel_id=1, source_target_pairs={{0,1},{1,2},{2,3},{3,4},{4,5},{5,6},{6,7},{7,8},{8,9},{9,10},{10,1... | collective-permute-start | bytes 196616 | tf_op jit(solution)/shard_map/ppermute | solution.py:269
  101.7 2.2 %collective-permute-start.3 = (bf16[64,512]{1,0:T(8,128)(2,1)S(1)}, bf16[64,512]{1,0:T(8,128)(2,1)S(1)}, u32[]{:S(2)}, u32[]{:S(2)}) collective-permute-start(bf16[64,512]{1,0:T(8,128)(2,1)S(1)} %get-tuple-element.36), channel_id=1, source_target_pairs={{1,0},{2,1},{3,2},{4,3},{5,4},{6,5},{7,6},{8,7},{9,8},{10,9},{11,1... | collective-permute-start | bytes 196616 | tf_op jit(solution)/shard_map/ppermute | solution.py:269
  103.9 3.2 %shard_map.242 = (bf16[512,512]{1,0:T(8,128)(2,1)}, f32[1536,512]{1,0:T(8,128)S(1)}, bf16[512,512]{1,0:T(8,128)(2,1)S(1)}, bf16[512,512]{1,0:T(8,128)(2,1)S(1)},...) custom-call(s32[1]{0:T(128)} %bitcast.off_ref, s32[3,512]{1,0:T(4,128)S(1)} %copy-done.6, ...), custom_call_target="tpu_custom_call" | custom-call | flops 1342177280 | bytes 4194304 | tf_op jit(solution)/shard_map/pallas_call | solution.py:360
  107.1 0.2 collective-permute-done.3.after_ref
  107.3 3.7 %shard_map.243 = bf16[100,512]{1,0:T(8,128)(2,1)} custom-call(s32[1]{0:T(128)} %bitcast.off_ref, s32[3,512]{1,0:T(4,128)S(1)} %copy-done.6, bf16[64,512]{1,0:T(8,128)(2,1)S(1)} %collective-permute-done.2.before_ref, bf16[64,512]{1,0:T(8,128)(2,1)S(1)} %collective-permute-done.3.after_ref, f32[1536,512]{1,0:T(8,128)S(1)} %get-tuple-element.37.pre_ref, ...), custom_call_target="tpu_custom_call" | custom-call | flops 1610612736 | bytes 4194304 | tf_op jit(solution)/shard_map/pallas_call | solution.py:383
  (37 shorter events, 0.2 us)
Async XLA Ops:
  0.6 81.1 %copy-start.11 = (s32[512]{0:T(512)S(1)}, s32[512]{0:T(512)}, u32[]{:S(2)}) copy-start(s32[512]{0:T(512)} %param.29) | copy-start | bytes 6148
  0.6 81.0 %copy-start.12 = (s32[512]{0:T(512)S(1)}, s32[512]{0:T(512)}, u32[]{:S(2)}) copy-start(s32[512]{0:T(512)} %param.30) | copy-start | bytes 6148
  0.7 81.3 %copy-start.9 = (f32[4,3,512]{2,0,1:T(4,128)S(1)}, f32[4,3,512]{2,0,1:T(4,128)}, u32[]{:S(2)}) copy-start(f32[4,3,512]{2,0,1:T(4,128)} %param.33) | copy-start | bytes 73732
  0.7 81.3 %copy-start.10 = (f32[4,512]{1,0:T(4,128)S(1)}, f32[4,512]{1,0:T(4,128)}, u32[]{:S(2)}) copy-start(f32[4,512]{1,0:T(4,128)} %param.31) | copy-start | bytes 24580
  0.7 81.6 %copy-start.4 = (f32[4,512]{1,0:T(4,128)S(1)}, f32[4,512]{1,0:T(4,128)}, u32[]{:S(2)}) copy-start(f32[4,512]{1,0:T(4,128)} %weg_ref.1) | copy-start | bytes 24580
  0.7 81.6 %copy-start.1 = (f32[4,2048]{1,0:T(4,128)S(1)}, f32[4,2048]{1,0:T(4,128)}, u32[]{:S(2)}) copy-start(f32[4,2048]{1,0:T(4,128)} %geo_ref.1) | copy-start | bytes 98308
  0.7 81.6 %copy-start.3 = (s32[2048]{0:T(1024)S(1)}, s32[2048]{0:T(1024)}, u32[]{:S(2)}) copy-start(s32[2048]{0:T(1024)} %param.27) | copy-start | bytes 24580
  0.7 81.6 %copy-start.2 = (s32[2048]{0:T(1024)S(1)}, s32[2048]{0:T(1024)}, u32[]{:S(2)}) copy-start(s32[2048]{0:T(1024)} %param.26) | copy-start | bytes 24580
  1.6 28.7 %collective-permute-start = (bf16[64,512]{1,0:T(8,128)(2,1)S(1)}, bf16[64,512]{1,0:T(8,128)(2,1)S(1)}, u32[]{:S(2)}, u32[]{:S(2)}) collective-permute-start(bf16[64,512]{1,0:T(8,128)(2,1)S(1)} %get-tuple-element.42), channel_id=1, source_target_pairs={{0,1},{1,2},{2,3},{3,4},{4,5},{5,6},{6,7},{7,8},{8,9},{9,10},{10,1... | collective-permute-start | bytes 196616 | tf_op jit(solution)/shard_map/ppermute | solution.py:269
  6.7 23.6 %collective-permute-start.1 = (bf16[64,512]{1,0:T(8,128)(2,1)S(1)}, bf16[64,512]{1,0:T(8,128)(2,1)S(1)}, u32[]{:S(2)}, u32[]{:S(2)}) collective-permute-start(bf16[64,512]{1,0:T(8,128)(2,1)S(1)} %get-tuple-element.22), channel_id=1, source_target_pairs={{1,0},{2,1},{3,2},{4,3},{5,4},{6,5},{7,6},{8,7},{9,8},{10,9},{11,1... | collective-permute-start | bytes 196616 | tf_op jit(solution)/shard_map/ppermute | solution.py:269
  26.9 44.7 %all-to-all-start = ((s32[8,8,128]{2,1,0:T(8,128)}), s32[8,8,128]{2,1,0:T(8,128)S(1)}, u32[]{:S(2)}, u32[]{:S(2)}) async-start(s32[8,8,128]{2,1,0:T(8,128)} %broadcast_in_dim.15), calls=%async_computation | async-start | bytes 65536 | tf_op jit(solution)/shard_map/all_to_all | solution.py:298
  72.9 23.1 %all-to-all-start.1 = ((bf16[8,64,512]{2,1,0:T(8,128)(2,1)}), bf16[8,64,512]{2,1,0:T(8,128)(2,1)S(1)}, u32[]{:S(2)}, u32[]{:S(2)}) async-start(bf16[8,64,512]{2,1,0:T(8,128)(2,1)} %bitcast.4), calls=%async_computation.1 | async-start | bytes 1048576 | tf_op jit(solution)/shard_map/all_to_all | solution.py:308
  93.2 0.8 copy-start.7
  94.0 0.8 copy-start.8
  94.8 9.0 %copy-start.5 = (f32[4,512]{1,0:T(4,128)S(1)}, f32[4,512]{1,0:T(4,128)}, u32[]{:S(2)}) copy-start(f32[4,512]{1,0:T(4,128)} %wdgeo_ref.1) | copy-start | bytes 24580
  94.8 9.0 %copy-start.6 = (s32[3,512]{1,0:T(4,128)S(1)}, s32[3,512]{1,0:T(4,128)}, u32[]{:S(2)}) copy-start(s32[3,512]{1,0:T(4,128)} %ds_ref.3) | copy-start | bytes 18436
  99.1 8.1 %copy-start = (bf16[100,512]{1,0:T(8,128)(2,1)S(1)}, bf16[100,512]{1,0:T(8,128)(2,1)}, u32[]{:S(2)}) copy-start(bf16[100,512]{1,0:T(8,128)(2,1)} %wp_ref.1) | copy-start | bytes 307204
  99.2 7.9 %collective-permute-start.2 = (bf16[64,512]{1,0:T(8,128)(2,1)S(1)}, bf16[64,512]{1,0:T(8,128)(2,1)S(1)}, u32[]{:S(2)}, u32[]{:S(2)}) collective-permute-start(bf16[64,512]{1,0:T(8,128)(2,1)S(1)} %get-tuple-element.35), channel_id=1, source_target_pairs={{0,1},{1,2},{2,3},{3,4},{4,5},{5,6},{6,7},{7,8},{8,9},{9,10},{10,1... | collective-permute-start | bytes 196616 | tf_op jit(solution)/shard_map/ppermute | solution.py:269
  101.7 5.6 %collective-permute-start.3 = (bf16[64,512]{1,0:T(8,128)(2,1)S(1)}, bf16[64,512]{1,0:T(8,128)(2,1)S(1)}, u32[]{:S(2)}, u32[]{:S(2)}) collective-permute-start(bf16[64,512]{1,0:T(8,128)(2,1)S(1)} %get-tuple-element.36), channel_id=1, source_target_pairs={{1,0},{2,1},{3,2},{4,3},{5,4},{6,5},{7,6},{8,7},{9,8},{10,9},{11,1... | collective-permute-start | bytes 196616 | tf_op jit(solution)/shard_map/ppermute | solution.py:269

commit v3 on v2

--- a/solution.py
+++ b/solution.py
@@ -95,8 +95,9 @@
 def fine_kernel(
     off_ref, fs_ref, sr_ref, geo_ref, lr_ref, lgeo_ref, before_ref, after_ref, weg_ref,
     x_hbm, ws_hbm, wr_hbm, wm_hbm, wself_hbm, grid_hbm, wdg_hbm, wgs_hbm,
-    agg_ref, base_ref, nself_ref, ws_ref, gproj_ref, gself_ref,
-    tab, msg, gsc, lsc, wsc, x_ref, wr_ref, wm_ref, wself_ref, grid_ref, wdg_ref, wgs_ref, sems, *, tile,
+    agg_ref, base_ref, nself_ref, ws_ref, gproj_hbm, gself_hbm,
+    tab, msg, gsc, lsc, wsc, x_ref, wr_ref, wm_ref, wself_ref, grid_ref, wdg_ref, wgs_ref,
+    gproj_ref, gself_ref, sems, out_sems, *, tile,
 ):
     x_copy, ws_copy, wr_copy, wm_copy, wself_copy, grid_copy, wdg_copy, wgs_copy = fetch(
         [
@@ -128,6 +129,7 @@
     gproj_ref[...] = dot(grid_ref[...], wdg_ref[...]).astype(BF16)
     wgs_copy.wait()
     gself_ref[...] = dot(grid_ref[...], wgs_ref[...]).astype(BF16)
+    stores = fetch([(gproj_ref, gproj_hbm), (gself_ref, gself_hbm)], out_sems)
     wm_copy.wait()
     off = off_ref[0]
     per = tile // LANES
@@ -152,6 +154,8 @@
     recv = columns([lr_ref[b : b + 1, :] for b in range(far)])
     lhs = jnp.concatenate([one_hot(recv, n), geo_columns(lsc[...])], axis=1)
     base_ref[...] = dot(lhs, tab[ext : ext + n + LANES, :]).astype(BF16)
+    for store in stores:
+        store.wait()
 
 
 def node_kernel(
@@ -313,15 +317,15 @@
     target = jnp.where(long_send >= 0, long_recv, -1)
     target = target.reshape(rings, BLOCK, slot).transpose(1, 0, 2).reshape(far // LANES, LANES)
     far_geo = long_geo.reshape(-1, rings, BLOCK, slot).transpose(0, 2, 1, 3).reshape(-1, far)
-    tile = 512
+    tile = 1024
     ext = n + 2 * BORDER
     dense = pltpu.VMEM((h, h), BF16)
-    field = jax.ShapeDtypeStruct((points, h), BF16)
+    field = pltpu.MemorySpace.HBM((points, h), BF16)
     aggregate, base, node_self, send_weight, grid_proj, grid_self = call(
         functools.partial(fine_kernel, tile=tile),
         (jax.ShapeDtypeStruct((n, h), F32), jax.ShapeDtypeStruct((far, h), BF16), whole, weight, field, field),
         [SM] + [VM] * 8 + [AN] * 8,
-        (VM,) * 6,
+        (VM,) * 4 + (AN,) * 2,
         [
             pltpu.VMEM((ext + n + LANES, h), BF16),
             pltpu.VMEM((edges, h), BF16),
@@ -332,7 +336,10 @@
             dense, dense, dense,
             pltpu.VMEM((points, h), BF16),
             dense, dense,
+            pltpu.VMEM((points, h), BF16),
+            pltpu.VMEM((points, h), BF16),
             pltpu.SemaphoreType.DMA((8,)),
+            pltpu.SemaphoreType.DMA((2,)),
         ],
         mib=28,
         flops=8 * edges * h * h,
@@ -361,7 +368,7 @@
         own_kernel,
         (
             whole, jax.ShapeDtypeStruct((vertices * points, h), F32),
-            field, weight, weight, weight,
+            jax.ShapeDtypeStruct((points, h), BF16), weight, weight, weight,
         ),
         [SM] + [VM] * 4 + [AN] * 5,
         (AN,) + (VM,) * 5,

time: 111 us -> 111 us (level)
  waiting for transfers between devices: 1.39 us -> 3.4 us
  local copies, waits for them, and re-layouts: 4.51 us -> 2.92 us
    all_to_all x1, waiting for transfers between devices: 1.21 us -> 3.38 us  [body(): lax.all_to_all(rows.reshape(BLOCK, far // BLOCK, h), 'region', split_axis...]
    unnamed x27 -> x23, local copies, waits for them, and re-layouts: 1.66 us -> 0.07 us
  transfers between devices with their start and end apart: 6 -> 6, of which waited for: 2 -> 1; matrix products, arithmetic and copies ran while one was open for 2% -> 2% of each run, Pallas kernels for 13% -> 12%
where the time goes in v3:
time: 111 us
  blocking collectives  41.3 us (37%)
  starting transfers between devices  40.6 us (37%)
  Pallas kernels  21.6 us (19%)
  waiting for transfers between devices  3.4 us (3%)
  local copies, waits for them, and re-layouts  2.92 us (3%)
    all_gather x1, blocking collectives, body(): lax.all_gather(head, 'region', axis=0, tiled=True, axis_index_groups=clas...  41.3 us
    ppermute x2, starting transfers between devices, swap(): lax.ppermute(first, 'region', down)  21.2 us
    pallas_call x1, Pallas kernels, body(): call(functools.partial(fine_kernel, tile=tile), (jax.ShapeDtypeStruct((n,...  10.4 us
    all_to_all x1, starting transfers between devices, body(): lax.all_to_all(rows.reshape(BLOCK, far // BLOCK, h), 'region', split_axis...  8.77 us
    ppermute x2, starting transfers between devices, swap(): lax.ppermute(last, 'region', up)  7.17 us
    pallas_call x1, Pallas kernels, body(): call(functools.partial(grid_kernel, nodes=n), jax.ShapeDtypeStruct((outpu...  3.72 us
    all_to_all x1, starting transfers between devices, body(): lax.all_to_all(wanted, 'region', split_axis=0, concat_axis=0, tiled=True,...  3.42 us
    all_to_all x1, waiting for transfers between devices, body(): lax.all_to_all(rows.reshape(BLOCK, far // BLOCK, h), 'region', split_axis...  3.38 us
  transfers between devices with their start and end apart: 6, of which 1 were waited for; matrix products, arithmetic and copies ran while one was open for 2% of the time, Pallas kernels for 12%

profile of v3, /device:TPU:37, one launch (start us, length us, event | category | flops | bytes accessed | tf_op | source)
XLA Modules:
  0.0 110.8 jit_solution(14209529286412486692)
XLA Ops:
  0.6 0.0 copy-start.9
  0.7 0.9 fusion.3
  1.6 5.1 %collective-permute-start = (bf16[64,512]{1,0:T(8,128)(2,1)S(1)}, bf16[64,512]{1,0:T(8,128)(2,1)S(1)}, u32[]{:S(2)}, u32[]{:S(2)}) collective-permute-start(bf16[64,512]{1,0:T(8,128)(2,1)S(1)} %get-tuple-element.42), channel_id=1, source_target_pairs={{0,1},{1,2},{2,3},{3,4},{4,5},{5,6},{6,7},{7,8},{8,9},{9,10},{10,1... | collective-permute-start | bytes 196616 | tf_op jit(solution)/shard_map/ppermute | solution.py:273
  6.7 18.6 %collective-permute-start.1 = (bf16[64,512]{1,0:T(8,128)(2,1)S(1)}, bf16[64,512]{1,0:T(8,128)(2,1)S(1)}, u32[]{:S(2)}, u32[]{:S(2)}) collective-permute-start(bf16[64,512]{1,0:T(8,128)(2,1)S(1)} %get-tuple-element.22), channel_id=1, source_target_pairs={{1,0},{2,1},{3,2},{4,3},{5,4},{6,5},{7,6},{8,7},{9,8},{10,9},{11,1... | collective-permute-start | bytes 196616 | tf_op jit(solution)/shard_map/ppermute | solution.py:273
  25.3 0.8 reshape.76
  26.1 0.1 add_bitcast_fusion
  26.2 0.1 reshape.77
  26.3 0.6 broadcast_in_dim.15
  26.9 3.4 %all-to-all-start = ((s32[8,8,128]{2,1,0:T(8,128)}), s32[8,8,128]{2,1,0:T(8,128)S(1)}, u32[]{:S(2)}, u32[]{:S(2)}) async-start(s32[8,8,128]{2,1,0:T(8,128)} %broadcast_in_dim.15), calls=%async_computation | async-start | bytes 65536 | tf_op jit(solution)/shard_map/all_to_all | solution.py:302
  30.4 41.3 %all_gather.3.table_ref = bf16[512,512]{1,0:T(8,128)(2,1)S(1)} all-gather(bf16[64,512]{1,0:T(8,128)(2,1)S(1)} %get-tuple-element.22), channel_id=1, replica_groups={{0,8,16,24,32,40,48,56},{1,9,17,25,33,41,49,57},{2,10,18,26,34,42,50,58..., dimensions={0}, use_global_device_ids=true | all-gather | bytes 589824 | tf_op jit(solution)/shard_map/all_gather | solution.py:307
  71.6 1.3 %shard_map.239 = bf16[512,512]{1,0:T(8,128)(2,1)} custom-call(s32[8,8,128]{2,1,0:T(8,128)S(1)} %all-to-all-done.asked_ref, bf16[512,512]{1,0:T(8,128)(2,1)S(1)} %all_gather.3.table_ref), custom_call_target="tpu_custom_call" | custom-call | bytes 4194304 | tf_op jit(solution)/shard_map/pallas_call | solution.py:310
  72.9 8.8 %all-to-all-start.1 = ((bf16[8,64,512]{2,1,0:T(8,128)(2,1)}), bf16[8,64,512]{2,1,0:T(8,128)(2,1)S(1)}, u32[]{:S(2)}, u32[]{:S(2)}) async-start(bf16[8,64,512]{2,1,0:T(8,128)(2,1)} %bitcast.4), calls=%async_computation.1 | async-start | bytes 1048576 | tf_op jit(solution)/shard_map/all_to_all | solution.py:312
  81.7 0.1 reshape.74
  81.8 0.1 reshape.75.lr_ref
  82.0 0.1 reshape.82
  82.1 0.1 reshape.83.lgeo_ref
  82.3 10.4 %shard_map.240 = (f32[512,512]{1,0:T(8,128)S(1)}, bf16[512,512]{1,0:T(8,128)(2,1)S(1)}, bf16[512,512]{1,0:T(8,128)(2,1)S(1)}, bf16[512,512]{1,0:T(8,128)(2,1)S(1...) custom-call(s32[1]{0:T(128)} %bitcast.off_ref, s32[16,128]{1,0:T(8,128)S(1)} %bitcast.16, s32[16,128]{1,0:T(8,128)S(1)} %bitcast.17, ...), custom_call_target="tpu_custom_call" | custom-call | flops 4294967296 | bytes 4194304 | tf_op jit(solution)/shard_map/pallas_call | solution.py:324
  92.6 0.0 copy-start.5
  92.7 3.4 %all-to-all-done.1 = bf16[8,64,512]{2,1,0:T(8,128)(2,1)S(1)} async-done(((bf16[8,64,512]{2,1,0:T(8,128)(2,1)}), bf16[8,64,512]{2,1,0:T(8,128)(2,1)S(1)}, u32[]{:S(2)}, u32[]{:S(2)}) %all-to-all-start.1) | async-done | bytes 524320 | tf_op jit(solution)/shard_map/all_to_all | solution.py:312
  96.1 3.1 %shard_map.241 = (bf16[512,512]{1,0:T(8,128)(2,1)S(1)}, bf16[64,512]{1,0:T(8,128)(2,1)S(1)}, bf16[64,512]{1,0:T(8,128)(2,1)S(1)}) custom-call(s32[4,128]{1,0:T(4,128)S(1)} %reshape.75.lr_ref, bf16[512,512]{1,0:T(8,128)(2,1)S(1)} %bitcast.15, f32[512,512]{1,0:T(8,128)S(1)} %get-tuple-element.27.agg_ref, bf16[512,512]{1,0:T(8,128)(2,1)S(1)} %get-tuple-element.28.base_ref, ...), custom_call_target="tpu_custom_call" | custom-call | flops 1342177280 | bytes 4194304 | tf_op jit(solution)/shard_map/pallas_call | solution.py:354
  99.2 2.1 %collective-permute-start.2 = (bf16[64,512]{1,0:T(8,128)(2,1)S(1)}, bf16[64,512]{1,0:T(8,128)(2,1)S(1)}, u32[]{:S(2)}, u32[]{:S(2)}) collective-permute-start(bf16[64,512]{1,0:T(8,128)(2,1)S(1)} %get-tuple-element.35), channel_id=1, source_target_pairs={{0,1},{1,2},{2,3},{3,4},{4,5},{5,6},{6,7},{7,8},{8,9},{9,10},{10,1... | collective-permute-start | bytes 196616 | tf_op jit(solution)/shard_map/ppermute | solution.py:273
  101.2 2.6 %collective-permute-start.3 = (bf16[64,512]{1,0:T(8,128)(2,1)S(1)}, bf16[64,512]{1,0:T(8,128)(2,1)S(1)}, u32[]{:S(2)}, u32[]{:S(2)}) collective-permute-start(bf16[64,512]{1,0:T(8,128)(2,1)S(1)} %get-tuple-element.36), channel_id=1, source_target_pairs={{1,0},{2,1},{3,2},{4,3},{5,4},{6,5},{7,6},{8,7},{9,8},{10,9},{11,1... | collective-permute-start | bytes 196616 | tf_op jit(solution)/shard_map/ppermute | solution.py:273
  103.9 3.2 %shard_map.242 = (bf16[512,512]{1,0:T(8,128)(2,1)}, f32[1536,512]{1,0:T(8,128)S(1)}, bf16[512,512]{1,0:T(8,128)(2,1)S(1)}, bf16[512,512]{1,0:T(8,128)(2,1)S(1)},...) custom-call(s32[1]{0:T(128)} %bitcast.off_ref, s32[3,512]{1,0:T(4,128)S(1)} %copy-done.6, ...), custom_call_target="tpu_custom_call" | custom-call | flops 1342177280 | bytes 4194304 | tf_op jit(solution)/shard_map/pallas_call | solution.py:367
  107.1 3.7 %shard_map.243 = bf16[100,512]{1,0:T(8,128)(2,1)} custom-call(s32[1]{0:T(128)} %bitcast.off_ref, s32[3,512]{1,0:T(4,128)S(1)} %copy-done.6, bf16[64,512]{1,0:T(8,128)(2,1)S(1)} %collective-permute-done.2.before_ref, bf16[64,512]{1,0:T(8,128)(2,1)S(1)} %collective-permute-done.3.after_ref, f32[1536,512]{1,0:T(8,128)S(1)} %get-tuple-element.37.pre_ref, ...), custom_call_target="tpu_custom_call" | custom-call | flops 1610612736 | bytes 4194304 | tf_op jit(solution)/shard_map/pallas_call | solution.py:390
  (33 shorter events, 0.2 us)
Async XLA Ops:
  0.6 81.1 %copy-start.9 = (s32[512]{0:T(512)S(1)}, s32[512]{0:T(512)}, u32[]{:S(2)}) copy-start(s32[512]{0:T(512)} %param.29) | copy-start | bytes 6148
  0.6 81.0 %copy-start.10 = (s32[512]{0:T(512)S(1)}, s32[512]{0:T(512)}, u32[]{:S(2)}) copy-start(s32[512]{0:T(512)} %param.30) | copy-start | bytes 6148
  0.7 81.3 %copy-start.7 = (f32[4,3,512]{2,0,1:T(4,128)S(1)}, f32[4,3,512]{2,0,1:T(4,128)}, u32[]{:S(2)}) copy-start(f32[4,3,512]{2,0,1:T(4,128)} %param.33) | copy-start | bytes 73732
  0.7 81.3 %copy-start.8 = (f32[4,512]{1,0:T(4,128)S(1)}, f32[4,512]{1,0:T(4,128)}, u32[]{:S(2)}) copy-start(f32[4,512]{1,0:T(4,128)} %param.31) | copy-start | bytes 24580
  0.7 81.6 %copy-start.4 = (f32[4,512]{1,0:T(4,128)S(1)}, f32[4,512]{1,0:T(4,128)}, u32[]{:S(2)}) copy-start(f32[4,512]{1,0:T(4,128)} %weg_ref.1) | copy-start | bytes 24580
  0.7 81.6 %copy-start.1 = (f32[4,2048]{1,0:T(4,128)S(1)}, f32[4,2048]{1,0:T(4,128)}, u32[]{:S(2)}) copy-start(f32[4,2048]{1,0:T(4,128)} %geo_ref.1) | copy-start | bytes 98308
  0.7 81.6 %copy-start.3 = (s32[2048]{0:T(1024)S(1)}, s32[2048]{0:T(1024)}, u32[]{:S(2)}) copy-start(s32[2048]{0:T(1024)} %param.27) | copy-start | bytes 24580
  0.7 81.6 %copy-start.2 = (s32[2048]{0:T(1024)S(1)}, s32[2048]{0:T(1024)}, u32[]{:S(2)}) copy-start(s32[2048]{0:T(1024)} %param.26) | copy-start | bytes 24580
  1.6 28.7 %collective-permute-start = (bf16[64,512]{1,0:T(8,128)(2,1)S(1)}, bf16[64,512]{1,0:T(8,128)(2,1)S(1)}, u32[]{:S(2)}, u32[]{:S(2)}) collective-permute-start(bf16[64,512]{1,0:T(8,128)(2,1)S(1)} %get-tuple-element.42), channel_id=1, source_target_pairs={{0,1},{1,2},{2,3},{3,4},{4,5},{5,6},{6,7},{7,8},{8,9},{9,10},{10,1... | collective-permute-start | bytes 196616 | tf_op jit(solution)/shard_map/ppermute | solution.py:273
  6.7 23.6 %collective-permute-start.1 = (bf16[64,512]{1,0:T(8,128)(2,1)S(1)}, bf16[64,512]{1,0:T(8,128)(2,1)S(1)}, u32[]{:S(2)}, u32[]{:S(2)}) collective-permute-start(bf16[64,512]{1,0:T(8,128)(2,1)S(1)} %get-tuple-element.22), channel_id=1, source_target_pairs={{1,0},{2,1},{3,2},{4,3},{5,4},{6,5},{7,6},{8,7},{9,8},{10,9},{11,1... | collective-permute-start | bytes 196616 | tf_op jit(solution)/shard_map/ppermute | solution.py:273
  26.9 44.7 %all-to-all-start = ((s32[8,8,128]{2,1,0:T(8,128)}), s32[8,8,128]{2,1,0:T(8,128)S(1)}, u32[]{:S(2)}, u32[]{:S(2)}) async-start(s32[8,8,128]{2,1,0:T(8,128)} %broadcast_in_dim.15), calls=%async_computation | async-start | bytes 65536 | tf_op jit(solution)/shard_map/all_to_all | solution.py:302
  72.9 23.1 %all-to-all-start.1 = ((bf16[8,64,512]{2,1,0:T(8,128)(2,1)}), bf16[8,64,512]{2,1,0:T(8,128)(2,1)S(1)}, u32[]{:S(2)}, u32[]{:S(2)}) async-start(bf16[8,64,512]{2,1,0:T(8,128)(2,1)} %bitcast.4), calls=%async_computation.1 | async-start | bytes 1048576 | tf_op jit(solution)/shard_map/all_to_all | solution.py:312
  92.6 11.2 %copy-start.5 = (f32[4,512]{1,0:T(4,128)S(1)}, f32[4,512]{1,0:T(4,128)}, u32[]{:S(2)}) copy-start(f32[4,512]{1,0:T(4,128)} %wdgeo_ref.1) | copy-start | bytes 24580
  92.7 11.2 %copy-start.6 = (s32[3,512]{1,0:T(4,128)S(1)}, s32[3,512]{1,0:T(4,128)}, u32[]{:S(2)}) copy-start(s32[3,512]{1,0:T(4,128)} %ds_ref.3) | copy-start | bytes 18436
  99.1 8.0 %copy-start = (bf16[100,512]{1,0:T(8,128)(2,1)S(1)}, bf16[100,512]{1,0:T(8,128)(2,1)}, u32[]{:S(2)}) copy-start(bf16[100,512]{1,0:T(8,128)(2,1)} %wp_ref.1) | copy-start | bytes 307204
  99.2 7.9 %collective-permute-start.2 = (bf16[64,512]{1,0:T(8,128)(2,1)S(1)}, bf16[64,512]{1,0:T(8,128)(2,1)S(1)}, u32[]{:S(2)}, u32[]{:S(2)}) collective-permute-start(bf16[64,512]{1,0:T(8,128)(2,1)S(1)} %get-tuple-element.35), channel_id=1, source_target_pairs={{0,1},{1,2},{2,3},{3,4},{4,5},{5,6},{6,7},{7,8},{8,9},{9,10},{10,1... | collective-permute-start | bytes 196616 | tf_op jit(solution)/shard_map/ppermute | solution.py:273
  101.2 5.9 %collective-permute-start.3 = (bf16[64,512]{1,0:T(8,128)(2,1)S(1)}, bf16[64,512]{1,0:T(8,128)(2,1)S(1)}, u32[]{:S(2)}, u32[]{:S(2)}) collective-permute-start(bf16[64,512]{1,0:T(8,128)(2,1)S(1)} %get-tuple-element.36), channel_id=1, source_target_pairs={{1,0},{2,1},{3,2},{4,3},{5,4},{6,5},{7,6},{8,7},{9,8},{10,9},{11,1... | collective-permute-start | bytes 196616 | tf_op jit(solution)/shard_map/ppermute | solution.py:273
